TPU v7x, 256 devices: a whole 4x4x8 slice. The times are simulated.
256 devices in a mesh: seq: 128 (over y, z_lo, x, core), par: 2 (over z_hi).
Axes of the slice: x: 4, y: 4, z: 8 (z_hi: 2, z_lo: 4; z = z_hi * 4 + z_lo), core: 2. Of those that a mesh axis runs over, the one named last changes fastest.
Arguments:
- states: float32 [32768, 128], P('seq'), may hold values from -6 to 6
- cotangent: float32 [32768, 128], P('seq'), may hold values from -6 to 6
- obs_count: int32 [256], P('seq'), may hold values from 16 to 128
- step_index: int32 [2, 32768], P(None, 'seq'), may hold values from 0 to 15
- step_table: float32 [16], replicated, may hold values from 0.05 to 0.25
- w_in: bfloat16 [128, 2048], P(None, 'par'), may hold values from -0.5 to 0.5
- b_hid: bfloat16 [2048], P('par'), may hold values from -3 to 3
- w_out: bfloat16 [128, 2048], P(None, 'par'), may hold values from -0.125 to 0.125
- b_out: float32 [128], replicated, may hold values from -3 to 3
Outputs:
- state_grad: float32 [32768, 128], P('seq')
- grad_in: float32 [128, 2048], P('seq', 'par')
- grad_out: float32 [128, 2048], P('seq', 'par')
All inputs are finite; a program needn't handle non-finite values.
Results may differ from a plain program's by a relative error of at most 0.0055.
Values may be sent and summed in bfloat16 or wider, within the bound.
No kernel may reach another device: no remote copies, remote signals or barrier semaphores. Data moves between devices by JAX's collectives and lax.ppermute only.
A program may use at most 64 MiB of HBM per device.

v0:
```python
import jax
import jax.numpy as jnp
from jax import lax
from jax.sharding import PartitionSpec as P

COEF_A = [
    [],
    [1.0 / 5],
    [3.0 / 40, 9.0 / 40],
    [44.0 / 45, -56.0 / 15, 32.0 / 9],
    [19372.0 / 6561, -25360.0 / 2187, 64448.0 / 6561, -212.0 / 729],
    [9017.0 / 3168, -355.0 / 33, 46732.0 / 5247, 49.0 / 176, -5103.0 / 18656],
]
COEF_B = [35.0 / 384, 0.0, 500.0 / 1113, 125.0 / 192, -2187.0 / 6784, 11.0 / 84]


def sent_to_all(value, axis):
    copies = jnp.broadcast_to(value, (lax.axis_size(axis), *value.shape))
    return lax.all_to_all(copies, axis, split_axis=0, concat_axis=0, tiled=True)


def laid_out(parts, dim):
    parts = jnp.moveaxis(parts, 0, dim)
    lengths = parts.shape
    return parts.reshape(*lengths[:dim], lengths[dim] * lengths[dim + 1], *lengths[dim + 2 :])


def collect(value, axis, dim):
    parts = sent_to_all(value, axis)
    return laid_out(parts, dim)


def side_by_side(arrays, axis, dim, along):
    ends, at = ([], 0)
    for a in arrays[:-1]:
        at += a.shape[along]
        ends.append(at)
    both = jnp.concatenate(arrays, axis=along)
    return tuple(jnp.split(collect(both, axis, dim), ends, axis=along))


def cut_along(value, dim, count):
    before, after = (value.shape[:dim], value.shape[dim + 1 :])
    return jnp.moveaxis(value.reshape(*before, count, -1, *after), dim, 0)


def sent_and_summed(value, axis, dim):
    parts = cut_along(value, dim, lax.axis_size(axis))
    arrived = lax.all_to_all(parts, axis, split_axis=0, concat_axis=0, tiled=True)
    return arrived.sum(axis=0)


def side_by_side_2(arrays, axis, dim, along):
    widths = [a.shape[along] for a in arrays]
    both = jnp.concatenate(arrays, axis=along)
    whole = sent_and_summed(both, axis, dim)
    return tuple(jnp.split(whole, [sum(widths[:k]) for k in range(1, len(widths))], axis=along))


def sum_packed(arrays, axis, dims):
    count = lax.axis_size(axis)
    parts = [cut_along(a, dim, count) for a, dim in zip(arrays, dims)]
    lines = jnp.concatenate([b.reshape(count, -1) for b in parts], axis=1)
    rows = max(16, -(-lines.shape[1] // 1024) * 8)
    lines = jnp.pad(lines, ((0, 0), (0, rows * 128 - lines.shape[1]))).reshape(-1, 128)
    ravelled, at, outs = (lax.psum_scatter(lines, axis, tiled=True).reshape(-1), 0, [])
    for b in parts:
        part = b[0]
        outs.append(ravelled[at : at + part.size].reshape(part.shape))
        at += part.size
    return tuple(outs)


def unchanged(value):
    return value


def field(state, w_in, b_hid, w_out, b_out, forward_sum):
    state_b = state.astype(jnp.bfloat16)
    hidden = jnp.tanh(
        jnp.dot(state_b, w_in, preferred_element_type=jnp.float32) + b_hid.astype(jnp.float32)
    )
    hidden_b = hidden.astype(jnp.bfloat16)
    partial_out = jnp.einsum("rh,lh->rl", hidden_b, w_out, preferred_element_type=jnp.float32)
    return (forward_sum(partial_out) + b_out, state_b, hidden, hidden_b)


def sweep(states, initial, sizes_list, w_in, b_hid, w_out, b_out, forward_sum, backward_sum):
    value = states
    records = []
    for size_now in sizes_list:
        slopes = []
        saved = []
        for current in range(6):
            if current == 0:
                probe = value
            else:
                combo = COEF_A[current][0] * slopes[0]
                for previous in range(1, current):
                    combo = combo + COEF_A[current][previous] * slopes[previous]
                probe = value + size_now * combo
            slope, state_b, hidden, hidden_b = field(probe, w_in, b_hid, w_out, b_out, forward_sum)
            slopes.append(slope)
            saved.append((state_b, hidden, hidden_b))
        combo = COEF_B[0] * slopes[0]
        for current in range(2, 6):
            combo = combo + COEF_B[current] * slopes[current]
        value = value + size_now * combo
        records.append((size_now, saved))
    back = initial
    grad_in = jnp.zeros(w_in.shape, jnp.float32)
    grad_out = jnp.zeros(w_out.shape, jnp.float32)
    for size_now, saved in reversed(records):
        adjoints = [None] * 6
        total = back
        for current in reversed(range(6)):
            combo = COEF_B[current] * back
            for later in range(current + 1, 6):
                combo = combo + COEF_A[later][current] * adjoints[later]
            grad_b = (size_now * combo).astype(jnp.bfloat16)
            state_b, hidden, hidden_b = saved[current]
            inner = jnp.dot(grad_b, w_out, preferred_element_type=jnp.float32) * (
                1.0 - hidden * hidden
            )
            inner_b = inner.astype(jnp.bfloat16)
            partial_back = jnp.einsum(
                "rh,lh->rl", inner_b, w_in, preferred_element_type=jnp.float32
            )
            adjoints[current] = backward_sum(partial_back)
            total = total + adjoints[current]
            grad_in = grad_in + jnp.einsum(
                "rl,rh->lh", state_b, inner_b, preferred_element_type=jnp.float32
            )
            grad_out = grad_out + jnp.einsum(
                "rl,rh->lh", grad_b, hidden_b, preferred_element_type=jnp.float32
            )
        back = total
    return (back, grad_in, grad_out)


def per_device(states, cotangent, obs_count, step_index, step_table, w_in, b_hid, w_out, b_out):
    rows = states.shape[0]
    local_seqs = obs_count.shape[0]
    slot_count = rows // local_seqs
    live = (jnp.arange(slot_count, dtype=jnp.int32)[None, :] < obs_count[:, None]).reshape(rows)
    initial = cotangent * live[:, None].astype(jnp.float32)
    table_ids = jnp.arange(step_table.shape[0], dtype=jnp.int32)

    def lookup(indices):
        picked = jnp.where(indices[:, None] == table_ids[None, :], step_table[None, :], 0.0)
        return jnp.sum(picked, axis=1)[:, None]

    first_size = lookup(step_index[0])
    second_size = lookup(step_index[1])
    whole_in, whole_out, whole_bias = side_by_side((w_in, w_out, b_hid[None, :]), "par", 1, 0)
    half = rows // lax.axis_size("par")
    start = lax.axis_index("par") * half

    def my_half(array):
        return lax.dynamic_slice_in_dim(array, start, half, 0)

    back, grad_in, grad_out = sweep(
        my_half(states),
        my_half(initial),
        (my_half(first_size), my_half(second_size)),
        whole_in,
        whole_bias[0],
        whole_out,
        b_out,
        unchanged,
        unchanged,
    )
    back = collect(back, "par", 0)
    grad_in, grad_out = side_by_side_2((grad_in, grad_out), "par", 1, 0)
    grad_in, grad_out = sum_packed((grad_in, grad_out), "seq", (0, 0))
    return (back, grad_in, grad_out)


def solution(mesh):
    return jax.shard_map(
        per_device,
        mesh=mesh,
        in_specs=(
            P("seq", None),
            P("seq", None),
            P("seq"),
            P(None, "seq"),
            P(),
            P(None, "par"),
            P("par"),
            P(None, "par"),
            P(),
        ),
        out_specs=(P("seq", None), P("seq", "par"), P("seq", "par")),
        check_vma=False,
    )
```

profile of v0, /device:TPU:1, one launch (start us, length us, event | category | flops | bytes accessed | tf_op | source)
XLA Modules:
  0.0 808.0 jit_solution(14727666258474221604)
XLA Ops:
  7.2 0.7 broadcast_in_dim.24
  7.9 1.1 pad_maximum_fusion.2
  9.0 1.1 broadcast_in_dim.25
  10.1 9.0 %all-to-all-start = ((bf16[2,257,1024]{2,1,0:T(8,128)(2,1)}), bf16[2,257,1024]{2,1,0:T(8,128)(2,1)S(1)}, u32[]{:S(2)}, u32[]{:S(2)}) async-start(bf16[2,257,1024]{2,1,0:T(8,128)(2,1)} %broadcast_in_dim.25), calls=%async_computation | async-start | bytes 2162688 | tf_op jit(solution)/shard_map/all_to_all | solution.py:19
  19.4 18.8 %all-to-all-done = bf16[2,257,1024]{2,1,0:T(8,128)(2,1)S(1)} async-done(((bf16[2,257,1024]{2,1,0:T(8,128)(2,1)}), bf16[2,257,1024]{2,1,0:T(8,128)(2,1)S(1)}, u32[]{:S(2)}, u32[]{:S(2)}) %all-to-all-start) | async-done | bytes 1052704 | tf_op jit(solution)/shard_map/all_to_all | solution.py:19
  38.3 0.8 copy.16
  39.5 0.5 copy-done.1
  47.4 0.3 fusion.12
  47.7 0.4 fusion.33
  49.1 0.3 convolution_add_fusion.10
  50.0 0.3 convolution_add_fusion.9
  51.0 0.3 convolution_add_fusion.8
  53.5 0.3 fusion.18
  53.8 0.4 convolution_add_fusion.5
  55.1 0.5 multiply_convert_fusion.3
  62.3 0.3 convolution_add_fusion.11
  63.1 21.2 %all_to_all.15 = f32[2,256,1024]{2,1,0:T(8,128)S(1)} all-to-all(f32[2,256,1024]{2,1,0:T(8,128)S(1)} %bitcast.180), channel_id=1, replica_groups=mesh['seq'=128,'par'=2] {'par'}, dimensions={0} | all-to-all | bytes 4194304 | tf_op jit(solution)/shard_map/all_to_all | solution.py:49
  84.4 1.2 reduce_sum.29
  85.6 1.3 fusion.63
  87.0 1.1 reshape.66
  88.4 29.8 %all_to_all.16 = f32[2,128,128]{2,1,0:T(8,128)S(1)} all-to-all(f32[2,128,128]{2,1,0:T(8,128)S(1)} %broadcast_in_dim.26), channel_id=1, replica_groups=mesh['seq'=128,'par'=2] {'par'}, dimensions={0} | all-to-all | bytes 262144 | tf_op jit(solution)/shard_map/all_to_all | solution.py:19
  118.3 681.0 %reduce-scatter.2.cloned.1.call-done = f32[16,128]{1,0:T(8,128)} async-done(((f32[2048,128]{1,0:T(8,128)}), f32[16,128]{1,0:T(8,128)}) %reduce-scatter.2.cloned.1.call-update) | async-done | bytes 8208 | tf_op jit(solution)/shard_map/reduce_scatter | solution.py:66
  799.3 1.3 fusion.64
  800.5 0.7 copy.25
  (89 shorter events, 20.5 us)
Async XLA Ops:
  8.9 10.2 %copy-start.5 = (s32[2]{0:T(128)S(1)}, s32[2]{0:T(128)}, u32[]{:S(2)}) copy-start(s32[2]{0:T(128)} %param.11) | copy-start | bytes 28
  8.9 10.3 %copy-start.3 = (s32[2,256]{1,0:T(2,128)S(1)}, s32[2,256]{1,0:T(2,128)}, u32[]{:S(2)}) copy-start(s32[2,256]{1,0:T(2,128)} %param.12) | copy-start | bytes 6148
  8.9 10.3 %copy-start.4 = (f32[16]{0:T(128)S(1)}, f32[16]{0:T(128)}, u32[]{:S(2)}) copy-start(f32[16]{0:T(128)} %param.13) | copy-start | bytes 196
  10.1 28.2 %all-to-all-start = ((bf16[2,257,1024]{2,1,0:T(8,128)(2,1)}), bf16[2,257,1024]{2,1,0:T(8,128)(2,1)S(1)}, u32[]{:S(2)}, u32[]{:S(2)}) async-start(bf16[2,257,1024]{2,1,0:T(8,128)(2,1)} %broadcast_in_dim.25), calls=%async_computation | async-start | bytes 2162688 | tf_op jit(solution)/shard_map/all_to_all | solution.py:19
  19.1 780.2 %reduce-scatter.2.cloned.1.call-start = ((), (), s32[]{:S(2)}) async-start(), calls=%async_computation.4 | async-start | bytes 1056768 | tf_op jit(solution)/shard_map/reduce_scatter | solution.py:66
  39.1 0.9 copy-start.1
  39.3 1.0 copy-start.2
  46.5 0.9 copy-start
Sparse Core Ops, SparseCore 0:
  88.2 710.9 reduce-scatter.1
where the time goes:
time: 813 us; the launch traced here: 808 us
  waiting for transfers between devices  700 us (86%)
  blocking collectives  51.1 us (6%)
  matrix products  22.2 us (3%)
  between operations  14.6 us (2%)
  starting transfers between devices  9 us (1%)
  local copies, waits for them, and re-layouts  8.3 us (1%)
    reduce_scatter x1, waiting for transfers between devices, sum_packed(): lax.psum_scatter(lines, axis, tiled=True).reshape(-1)  681 us
    all_to_all x1, blocking collectives, sent_to_all(): return lax.all_to_all(copies, axis, split_axis=0, concat_axis=0, tiled=True)  29.8 us
    all_to_all x1, blocking collectives, sent_and_summed(): lax.all_to_all(parts, axis, split_axis=0, concat_axis=0, tiled=True)  21.2 us
    all_to_all x1, waiting for transfers between devices, sent_to_all(): return lax.all_to_all(copies, axis, split_axis=0, concat_axis=0, tiled=True)  18.8 us
  transfers between devices with their start and end apart: 2, of which 2 were waited for; matrix products, arithmetic and copies ran while one was open for 0% of the time, Pallas kernels for 0%

commit v1 on v0

v1 whole, which is shorter than its diff:
```python
import jax
import jax.numpy as jnp
import numpy as np
from jax import lax
from jax.sharding import Mesh
from jax.sharding import PartitionSpec as P

SEQ = ("y", "z", "x", "core")
PLACE = SEQ + ("par",)
SIZES = (4, 4, 4, 2, 2)


def swapped(value, axis):
    at = PLACE.index(axis)
    pairs = []
    for source in range(int(np.prod(SIZES))):
        place = list(np.unravel_index(source, SIZES))
        place[at] = 1 - place[at]
        pairs.append((source, int(np.ravel_multi_index(place, SIZES))))
    return lax.ppermute(value, PLACE, pairs)

COEF_A = [
    [],
    [1.0 / 5],
    [3.0 / 40, 9.0 / 40],
    [44.0 / 45, -56.0 / 15, 32.0 / 9],
    [19372.0 / 6561, -25360.0 / 2187, 64448.0 / 6561, -212.0 / 729],
    [9017.0 / 3168, -355.0 / 33, 46732.0 / 5247, 49.0 / 176, -5103.0 / 18656],
]
COEF_B = [35.0 / 384, 0.0, 500.0 / 1113, 125.0 / 192, -2187.0 / 6784, 11.0 / 84]


def field(state, w_in, b_hid, w_out, b_out):
    state_b = state.astype(jnp.bfloat16)
    hidden = jnp.tanh(
        jnp.dot(state_b, w_in, preferred_element_type=jnp.float32) + b_hid.astype(jnp.float32)
    )
    hidden_b = hidden.astype(jnp.bfloat16)
    partial_out = jnp.einsum("rh,lh->rl", hidden_b, w_out, preferred_element_type=jnp.float32)
    return (partial_out + b_out, state_b, hidden, hidden_b)


def sweep(states, initial, sizes_list, w_in, b_hid, w_out, b_out, own):
    value = states
    records = []
    for size_now in sizes_list:
        slopes = []
        saved = []
        for current in range(6):
            if current == 0:
                probe = value
            else:
                combo = COEF_A[current][0] * slopes[0]
                for previous in range(1, current):
                    combo = combo + COEF_A[current][previous] * slopes[previous]
                probe = value + size_now * combo
            slope, state_b, hidden, hidden_b = field(probe, w_in, b_hid, w_out, b_out)
            slopes.append(slope)
            saved.append((state_b, hidden, hidden_b))
        combo = COEF_B[0] * slopes[0]
        for current in range(2, 6):
            combo = combo + COEF_B[current] * slopes[current]
        value = value + size_now * combo
        records.append((size_now, saved))
    back = initial
    grad_in = jnp.zeros((w_in.shape[0], own), jnp.float32)
    grad_out = jnp.zeros((w_in.shape[0], own), jnp.float32)
    for size_now, saved in reversed(records):
        adjoints = [None] * 6
        total = back
        for current in reversed(range(6)):
            combo = COEF_B[current] * back
            for later in range(current + 1, 6):
                combo = combo + COEF_A[later][current] * adjoints[later]
            grad_b = (size_now * combo).astype(jnp.bfloat16)
            state_b, hidden, hidden_b = saved[current]
            inner = jnp.dot(grad_b, w_out, preferred_element_type=jnp.float32) * (
                1.0 - hidden * hidden
            )
            inner_b = inner.astype(jnp.bfloat16)
            partial_back = jnp.einsum(
                "rh,lh->rl", inner_b, w_in, preferred_element_type=jnp.float32
            )
            adjoints[current] = partial_back
            total = total + adjoints[current]
            grad_in = grad_in + jnp.einsum(
                "rl,rh->lh", state_b, inner_b[:, :own], preferred_element_type=jnp.float32
            )
            grad_out = grad_out + jnp.einsum(
                "rl,rh->lh", grad_b, hidden_b[:, :own], preferred_element_type=jnp.float32
            )
        back = total
    return (back, grad_in, grad_out)


def per_device(states, cotangent, obs_count, step_index, step_table, w_in, b_hid, w_out, b_out):
    rows = states.shape[0]
    local_seqs = obs_count.shape[0]
    slot_count = rows // local_seqs
    live = (jnp.arange(slot_count, dtype=jnp.int32)[None, :] < obs_count[:, None]).reshape(rows)
    initial = cotangent * live[:, None].astype(jnp.float32)
    table_ids = jnp.arange(step_table.shape[0], dtype=jnp.int32)

    def lookup(indices):
        picked = jnp.where(indices[:, None] == table_ids[None, :], step_table[None, :], 0.0)
        return jnp.sum(picked, axis=1)[:, None]

    first_size = lookup(step_index[0])
    second_size = lookup(step_index[1])
    core = lax.axis_index("core")
    feats, own = w_in.shape
    mine = jnp.concatenate(
        [jnp.where(core == 0, w_in, w_out), jnp.broadcast_to(b_hid[None, :], (8, own))], axis=0
    )
    other = lax.all_gather(swapped(mine, "par"), "core")
    whole_in = jnp.concatenate([w_in, other[0, :feats]], axis=1)
    whole_out = jnp.concatenate([w_out, other[1, :feats]], axis=1)
    whole_bias = jnp.concatenate([b_hid, other[0, feats]])
    back, grad_in, grad_out = sweep(
        states, initial, (first_size, second_size), whole_in, whole_bias, whole_out, b_out, own
    )
    both = jnp.concatenate([grad_in, grad_out], axis=1).reshape(feats // 2, 2, 2 * own // 128, 128)
    keep = lax.dynamic_index_in_dim(both, core, 1, keepdims=False)
    send = lax.dynamic_index_in_dim(both, 1 - core, 1, keepdims=False)
    pair = (keep + swapped(send, "core")).astype(jnp.bfloat16)
    arrived = lax.all_to_all(pair, ("y", "z", "x"), split_axis=0, concat_axis=0, tiled=True)
    total = arrived.astype(jnp.float32).sum(axis=0).reshape(2, 1, own)
    return (back, total[0], total[1])


def solution(mesh):
    fine = Mesh(mesh.devices.reshape(SIZES), PLACE)
    return jax.shard_map(
        per_device,
        mesh=fine,
        in_specs=(
            P(SEQ, None),
            P(SEQ, None),
            P(SEQ),
            P(None, SEQ),
            P(),
            P(None, "par"),
            P("par"),
            P(None, "par"),
            P(),
        ),
        out_specs=(P(SEQ, None), P(SEQ, "par"), P(SEQ, "par")),
        check_vma=False,
    )
```

time: 813 us -> 79.7 us (0.10)
  waiting for transfers between devices: 700 us -> 15.5 us
  blocking collectives: 51.1 us -> 3.66 us
  between operations: 14.6 us -> 1.22 us
  starting transfers between devices: 9 us -> 22 us
    reduce_scatter x1 -> x0, waiting for transfers between devices: 681 us -> none  [sum_packed(): lax.psum_scatter(lines, axis, tiled=True).reshape(-1)]
    all_to_all x2 -> x0, blocking collectives: 51.1 us -> none  [the longest x1 29.8 us: sent_to_all(): return lax.all_to_all(copies, axis, split_axis=0, concat_axis=0, tiled=True)]
    all_to_all x1, waiting for transfers between devices: 18.8 us -> 9.12 us  [per_device(): lax.all_to_all(pair, ('y', 'z', 'x'), split_axis=0, concat_axis=0, tiled=...]
    ppermute x0 -> x2, starting transfers between devices: none -> 8.18 us  [swapped(): return lax.ppermute(value, PLACE, pairs)]
  transfers between devices with their start and end apart: 2 -> 3, of which waited for: 2 -> 3; matrix products, arithmetic and copies ran while one was open for 0% -> 6% of each run, Pallas kernels for 0% -> 0%
where the time goes in v1:
time: 79.7 us; the launch traced here: 79.4 us
  matrix products  29.9 us (38%)
  starting transfers between devices  22 us (28%)
  waiting for transfers between devices  15.5 us (19%)
  blocking collectives  3.66 us (5%)
  other arithmetic  3.6 us (5%)
  local copies, waits for them, and re-layouts  3.43 us (4%)
  between operations  1.22 us (2%)
    all_to_all x1, starting transfers between devices, per_device(): lax.all_to_all(pair, ('y', 'z', 'x'), split_axis=0, concat_axis=0, tiled=...  13.9 us
    all_to_all x1, waiting for transfers between devices, per_device(): lax.all_to_all(pair, ('y', 'z', 'x'), split_axis=0, concat_axis=0, tiled=...  9.12 us
    ppermute x2, starting transfers between devices, swapped(): return lax.ppermute(value, PLACE, pairs)  8.18 us
    dot_general x12, matrix products, sweep(): jnp.einsum('rh,lh->rl', inner_b, w_in, preferred_element_type=jnp.float32)  7.73 us
    ppermute x2, waiting for transfers between devices, swapped(): return lax.ppermute(value, PLACE, pairs)  6.43 us
    dot_general x12, matrix products, sweep(): jnp.dot(grad_b, w_out, preferred_element_type=jnp.float32)  5.31 us
    dot_general x12, matrix products, field(): jnp.dot(state_b, w_in, preferred_element_type=jnp.float32)  5.28 us
    dot_general x11, matrix products, field(): jnp.einsum('rh,lh->rl', hidden_b, w_out, preferred_element_type=jnp.float32)  5.02 us
  transfers between devices with their start and end apart: 3, of which 3 were waited for; matrix products, arithmetic and copies ran while one was open for 6% of the time, Pallas kernels for 0%

profile of v1, /device:TPU:1, one launch (start us, length us, event | category | flops | bytes accessed | tf_op | source)
XLA Modules:
  0.0 79.4 jit_solution(7554797843443842550)
XLA Ops:
  0.7 1.0 %broadcast_select_fusion = bf16[128,1024]{1,0:T(8,128)(2,1)S(1)} fusion(bf16[128,1024]{1,0:T(8,128)(2,1)} %param.14, bf16[128,1024]{1,0:T(8,128)(2,1)} %param.16, pred[]{:T(512)S(6)} %eq.37), kind=kLoop, calls=%fused_computation.131 | loop fusion | flops 131072 | bytes 786433 | tf_op jit(solution)/shard_map/jit(_where)/select_n | solution.py:113
  1.7 0.7 broadcast_in_dim.20
  2.4 7.8 %collective-permute-start = (bf16[136,1024]{1,0:T(8,128)(2,1)S(1)}, bf16[136,1024]{1,0:T(8,128)(2,1)S(1)}, u32[]{:S(2)}, u32[]{:S(2)}) collective-permute-start(bf16[136,1024]{1,0:T(8,128)(2,1)S(1)} %pad_maximum_fusion.2), channel_id=1, source_target_pairs={{0,1},{1,0},{2,3},{3,2},{4,5},{5,4},{6,7},{7,6},{8,9},{9,8},{10,11... | collective-permute-start | bytes 835592 | tf_op jit(solution)/shard_map/ppermute | solution.py:20
  10.2 0.8 fusion.77
  11.0 0.7 fusion.65
  11.7 0.7 select_reduce_fusion.1
  12.5 4.7 %collective-permute-done = bf16[136,1024]{1,0:T(8,128)(2,1)S(1)} collective-permute-done((bf16[136,1024]{1,0:T(8,128)(2,1)S(1)}, bf16[136,1024]{1,0:T(8,128)(2,1)S(1)}, u32[]{:S(2)}, u32[]{:S(2)}) %collective-permute-start) | collective-permute-done | bytes 278560 | tf_op jit(solution)/shard_map/ppermute | solution.py:20
  17.1 3.7 %all-gather = bf16[272,1024]{1,0:T(8,128)(2,1)S(1)} all-gather(bf16[136,1024]{1,0:T(8,128)(2,1)S(1)} %collective-permute-done), channel_id=2, replica_groups=mesh['y'=4,'z'=4,'x'=4,'core'=2,'par'=2] {'core'}, dimensions={0}, use_global_device_ids=true | all-gather | bytes 835584 | tf_op jit(solution)/shard_map/all_gather | solution.py:115
  20.9 0.6 fusion.11
  21.7 0.5 add_convert_fusion.8
  24.5 0.5 add_convert_fusion.5
  29.8 0.5 add_convert_fusion
  31.6 0.5 fusion.12
  38.7 0.5 convolution_add_fusion.34
  39.2 0.5 fusion.18
  44.5 1.1 %multiply_convert_fusion = (bf16[256,128]{1,0:T(8,128)(2,1)S(1)}, f32[256,128]{1,0:T(8,128)}) fusion(f32[256,128]{1,0:T(8,128)S(1)} %get-tuple-element.64, f32[256,128]{1,0:T(8,128)S(1)} %get-tuple-element.66, f32[256,128]{1,0:T(8,128)S(1)} %get-tuple-element.68, f32[256,128]{1,0:T(8,128)S(1)} %get-tuple-element.70, ...), kind=kOutput, calls=%fused_computation.132 | convolution fusion | flops 135692288 | bytes 2425856 | tf_op jit(solution)/shard_map/rh,lh->rl/dot_general | solution.py:81
  45.6 0.5 fusion.23
  49.8 0.8 %dynamic-slice_bitcast_fusion = f32[64,16,128]{2,1,0:T(8,128)} fusion(f32[64,2,16,128]{3,2,1,0:T(8,128)S(1)} %bitcast.91, s32[]{:T(128)S(6)} %select_n.27), kind=kLoop, calls=%fused_computation.125 | loop fusion | bytes 1048580 | tf_op jit(solution)/shard_map/jit(dynamic_index_in_dim)/squeeze | solution.py:124
  51.0 1.8 %collective-permute-done.1 = f32[64,16,128]{2,1,0:T(8,128)S(1)} collective-permute-done((f32[64,16,128]{2,1,0:T(8,128)}, f32[64,16,128]{2,1,0:T(8,128)S(1)}, u32[]{:S(2)}, u32[]{:S(2)}) %collective-permute-start.1) | collective-permute-done | bytes 524320 | tf_op jit(solution)/shard_map/ppermute | solution.py:20
  52.8 0.8 %fusion.59 = bf16[64,16,128]{2,1,0:T(8,128)(2,1)} fusion(f32[64,16,128]{2,1,0:T(8,128)S(1)} %collective-permute-done.1, f32[64,2,16,128]{3,2,1,0:T(8,128)S(1)} %bitcast.92, s32[]{:T(128)S(6)} %select_n.26), kind=kLoop, calls=%fused_computation.123 | loop fusion | flops 262144 | bytes 1310724 | tf_op jit(solution)/shard_map/convert_element_type | solution.py:125
  53.6 13.9 %all-to-all-start = ((bf16[64,16,128]{2,1,0:T(8,128)(2,1)}), bf16[64,16,128]{2,1,0:T(8,128)(2,1)S(1)}, u32[]{:S(2)}, u32[]{:S(2)}) async-start(bf16[64,16,128]{2,1,0:T(8,128)(2,1)} %fusion.59), calls=%async_computation | async-start | bytes 524288 | tf_op jit(solution)/shard_map/all_to_all | solution.py:126
  67.4 2.2 %convolution_add_fusion.33 = f32[256,128]{1,0:T(8,128)} fusion(bf16[256,2048]{0,1:T(8,128)(2,1)S(1)} %fusion.23, f32[256,128]{1,0:T(8,128)} %get-tuple-element.72, f32[256,128]{1,0:T(8,128)} %copy-done.5, f32[256,128]{1,0:T(8,128)} %copy-done.4, f32[256,128]{1,0:T(8,128)S(1)} %get-tuple-element.66, f32[256,128]{1,0:T(8,128)S(1)} %convolution_add_fusion.34, ...), kind=kOutput, calls=%fused_computation.71 | convolution fusion | flops 135462912 | bytes 2490368 | tf_op jit(solution)/shard_map/rh,lh->rl/dot_general | solution.py:81
  69.6 9.1 %all-to-all-done = bf16[64,16,128]{2,1,0:T(8,128)(2,1)S(1)} async-done(((bf16[64,16,128]{2,1,0:T(8,128)(2,1)}), bf16[64,16,128]{2,1,0:T(8,128)(2,1)S(1)}, u32[]{:S(2)}, u32[]{:S(2)}) %all-to-all-start) | async-done | bytes 262176 | tf_op jit(solution)/shard_map/all_to_all | solution.py:126
  78.8 0.6 fusion.76
  (87 shorter events, 23.9 us)
Async XLA Ops:
  0.6 20.3 %copy-start = (bf16[128,1024]{1,0:T(8,128)(2,1)S(1)}, bf16[128,1024]{1,0:T(8,128)(2,1)}, u32[]{:S(2)}) copy-start(bf16[128,1024]{1,0:T(8,128)(2,1)} %param.14) | copy-start | bytes 786436
  0.6 20.2 %copy-start.6 = (bf16[1024]{0:T(1024)(128)(2,1)S(1)}, bf16[1024]{0:T(1024)(128)(2,1)}, u32[]{:S(2)}) copy-start(bf16[1024]{0:T(1024)(128)(2,1)} %param.15) | copy-start | bytes 6148
  0.7 20.2 %copy-start.2 = (f32[256,128]{1,0:T(8,128)S(1)}, f32[256,128]{1,0:T(8,128)}, u32[]{:S(2)}) copy-start(f32[256,128]{1,0:T(8,128)} %param.9) | copy-start | bytes 393220
  2.4 14.7 %collective-permute-start = (bf16[136,1024]{1,0:T(8,128)(2,1)S(1)}, bf16[136,1024]{1,0:T(8,128)(2,1)S(1)}, u32[]{:S(2)}, u32[]{:S(2)}) collective-permute-start(bf16[136,1024]{1,0:T(8,128)(2,1)S(1)} %pad_maximum_fusion.2), channel_id=1, source_target_pairs={{0,1},{1,0},{2,3},{3,2},{4,5},{5,4},{6,7},{7,6},{8,9},{9,8},{10,11... | collective-permute-start | bytes 835592 | tf_op jit(solution)/shard_map/ppermute | solution.py:20
  20.8 0.9 %copy-start.1 = (bf16[128,1024]{1,0:T(8,128)(2,1)S(1)}, bf16[128,1024]{1,0:T(8,128)(2,1)}, u32[]{:S(2)}) copy-start(bf16[128,1024]{1,0:T(8,128)(2,1)} %param.16) | copy-start | bytes 786436
  20.8 1.0 %copy-start.7 = (f32[128]{0:T(128)S(1)}, f32[128]{0:T(128)}, u32[]{:S(2)}) copy-start(f32[128]{0:T(128)} %param.17) | copy-start | bytes 1540
  30.7 0.9 %copy-start.3 = (f32[256,128]{1,0:T(8,128)S(1)}, f32[256,128]{1,0:T(8,128)}, u32[]{:S(2)}) copy-start(f32[256,128]{1,0:T(8,128)} %param.10) | copy-start | bytes 393220
  42.7 1.9 %copy-start.4 = (f32[256,128]{1,0:T(8,128)}, f32[256,128]{1,0:T(8,128)S(1)}, u32[]{:S(2)}) copy-start(f32[256,128]{1,0:T(8,128)S(1)} %get-tuple-element.68) | copy-start | bytes 393220
  43.8 2.6 %copy-start.5 = (f32[256,128]{1,0:T(8,128)}, f32[256,128]{1,0:T(8,128)S(1)}, u32[]{:S(2)}) copy-start(f32[256,128]{1,0:T(8,128)S(1)} %get-tuple-element.70) | copy-start | bytes 393220
  50.6 2.1 %collective-permute-start.1 = (f32[64,16,128]{2,1,0:T(8,128)}, f32[64,16,128]{2,1,0:T(8,128)S(1)}, u32[]{:S(2)}, u32[]{:S(2)}) collective-permute-start(f32[64,16,128]{2,1,0:T(8,128)} %dynamic-slice_bitcast_fusion), channel_id=1, source_target_pairs={{0,2},{1,3},{2,0},{3,1},{4,6},{5,7},{6,4},{7,5},{8,10},{9,11},{10,... | collective-permute-start | bytes 1572872 | tf_op jit(solution)/shard_map/ppermute | solution.py:20
  53.6 25.2 %all-to-all-start = ((bf16[64,16,128]{2,1,0:T(8,128)(2,1)}), bf16[64,16,128]{2,1,0:T(8,128)(2,1)S(1)}, u32[]{:S(2)}, u32[]{:S(2)}) async-start(bf16[64,16,128]{2,1,0:T(8,128)(2,1)} %fusion.59), calls=%async_computation | async-start | bytes 524288 | tf_op jit(solution)/shard_map/all_to_all | solution.py:126

commit v2 on v1

v2 whole, which is shorter than its diff:
```python
import jax
import jax.numpy as jnp
import numpy as np
from jax import lax
from jax.experimental import pallas as pl
from jax.experimental.pallas import tpu as pltpu
from jax.sharding import Mesh
from jax.sharding import PartitionSpec as P

SEQ = ("y", "z", "x", "core")
PLACE = SEQ + ("par",)
SIZES = (4, 4, 4, 2, 2)


def swapped(value, axis):
    at = PLACE.index(axis)
    pairs = []
    for source in range(int(np.prod(SIZES))):
        place = list(np.unravel_index(source, SIZES))
        place[at] = 1 - place[at]
        pairs.append((source, int(np.ravel_multi_index(place, SIZES))))
    return lax.ppermute(value, PLACE, pairs)

COEF_A = [
    [],
    [1.0 / 5],
    [3.0 / 40, 9.0 / 40],
    [44.0 / 45, -56.0 / 15, 32.0 / 9],
    [19372.0 / 6561, -25360.0 / 2187, 64448.0 / 6561, -212.0 / 729],
    [9017.0 / 3168, -355.0 / 33, 46732.0 / 5247, 49.0 / 176, -5103.0 / 18656],
]
COEF_B = [35.0 / 384, 0.0, 500.0 / 1113, 125.0 / 192, -2187.0 / 6784, 11.0 / 84]
BLOCK = 256
F32, BF16 = jnp.float32, jnp.bfloat16


def dot(a, b, contract=(1, 0)):
    dims = (((contract[0],), (contract[1],)), ((), ()))
    return lax.dot_general(a, b, dims, preferred_element_type=F32)


def transposed(value):
    rows, columns = value.shape
    return jnp.concatenate(
        [
            jnp.concatenate([value[i : i + 128, j : j + 128].T for i in range(0, rows, 128)], axis=1)
            for j in range(0, columns, 128)
        ],
        axis=0,
    )


def sweep_kernel(
    core, states, initial, sizes, bias_out, in_own, out_own, bias_own, other,
    back, keep, send,
    in_t, out_t, hid, slope_of, probe, value, terms, acc_in, acc_out, square,
):
    feats, own = in_own.shape
    rows = states.shape[0]
    in_other, out_other, bias_other = other.at[0, :feats], other.at[1, :feats], other.at[0, feats:]
    for half, (w_in, w_out, bias) in enumerate(
        ((in_own, out_own, bias_own), (in_other, out_other, bias_other))
    ):
        for at in range(0, own, 128):
            to = pl.ds(half * own + at, 128)
            in_t[to, :feats] = w_in[:, at : at + 128].T
            low = jnp.concatenate(
                [bias[:, at : at + 128].astype(F32), jnp.zeros((128 - bias.shape[0], 128), F32)]
            )
            in_t[to, feats:] = low.T.astype(BF16)
            out_t[to, :] = w_out[:, at : at + 128].T
    value[...] = transposed(states[...])
    acc_in[...] = jnp.zeros_like(acc_in)
    acc_out[...] = jnp.zeros_like(acc_out)
    unit = jnp.where(lax.broadcasted_iota(jnp.int32, (feats, rows), 0) == 0, 1.0, 0.0).astype(BF16)
    bias_o = bias_out[...]

    def forward(step, _):
        size = sizes[step]
        for now in range(6):
            state = value[...]
            if now:
                combo = COEF_A[now][0] * terms[0]
                for before in range(1, now):
                    combo = combo + COEF_A[now][before] * terms[before]
                state = state + size * combo
            state_b = state.astype(BF16)
            probe[step, now] = state_b
            full = jnp.concatenate([state_b, unit], axis=0)
            for at in range(0, 2 * own, BLOCK):
                hidden = jnp.tanh(dot(in_t[at : at + BLOCK], full))
                hid[step, now, at : at + BLOCK] = hidden.astype(BF16)
                slope_of[step, now, at : at + BLOCK] = (1.0 - hidden * hidden).astype(BF16)
            terms[now] = (
                dot(out_own[...], hid[step, now, :own])
                + dot(out_other[...], hid[step, now, own:])
                + bias_o
            )
        combo = COEF_B[0] * terms[0]
        for now in range(2, 6):
            combo = combo + COEF_B[now] * terms[now]
        value[...] = value[...] + size * combo
        return 0

    lax.fori_loop(0, 2, forward, 0)
    value[...] = transposed(initial[...])

    def backward(turn, _):
        step = 1 - turn
        size = sizes[step]
        for now in reversed(range(6)):
            combo = COEF_B[now] * value[...]
            for later in range(now + 1, 6):
                combo = combo + COEF_A[later][now] * terms[later]
            grad_b = (size * combo).astype(BF16)
            for at in range(0, 2 * own, BLOCK):
                inner = dot(out_t[at : at + BLOCK], grad_b) * slope_of[
                    step, now, at : at + BLOCK
                ].astype(F32)
                slope_of[step, now, at : at + BLOCK] = inner.astype(BF16)
            terms[now] = dot(in_own[...], slope_of[step, now, :own]) + dot(
                in_other[...], slope_of[step, now, own:]
            )
            acc_in[...] += dot(slope_of[step, now, :own], probe[step, now], (1, 1))
            acc_out[...] += dot(hid[step, now, :own], grad_b, (1, 1))
        total = value[...]
        for now in reversed(range(6)):
            total = total + terms[now]
        value[...] = total
        return 0

    lax.fori_loop(0, 2, backward, 0)
    back[...] = transposed(value[...])
    tiles = own // 128
    for which, acc in enumerate((acc_in, acc_out)):
        for tile in range(tiles):
            at = which * tiles + tile
            square[at] = acc[tile * 128 : (tile + 1) * 128].T
    for side in range(2):

        @pl.when(core[0] == side)
        def _():
            for at in range(2 * tiles):
                line = pl.ds(at, feats // 2, stride=2 * tiles)
                keep[line, :] = square[at, pl.ds(side, feats // 2, stride=2), :]
                send[line, :] = square[at, pl.ds(1 - side, feats // 2, stride=2), :]


def run_sweep(core, states, initial, sizes, bias_out, in_own, out_own, bias_own, other):
    rows, feats = states.shape
    own = in_own.shape[1]
    lines = feats * own // 128
    space = pl.BlockSpec(memory_space=pltpu.VMEM)
    return pl.pallas_call(
        sweep_kernel,
        out_shape=(
            jax.ShapeDtypeStruct((rows, feats), F32),
            jax.ShapeDtypeStruct((lines, 128), F32),
            jax.ShapeDtypeStruct((lines, 128), F32),
        ),
        in_specs=[pl.BlockSpec(memory_space=pltpu.SMEM)] + [space] * 8,
        out_specs=(space,) * 3,
        scratch_shapes=[
            pltpu.VMEM((2 * own, 2 * feats), BF16),
            pltpu.VMEM((2 * own, feats), BF16),
            pltpu.VMEM((2, 6, 2 * own, rows), BF16),
            pltpu.VMEM((2, 6, 2 * own, rows), BF16),
            pltpu.VMEM((2, 6, feats, rows), BF16),
            pltpu.VMEM((feats, rows), F32),
            pltpu.VMEM((6, feats, rows), F32),
            pltpu.VMEM((own, feats), F32),
            pltpu.VMEM((own, feats), F32),
            pltpu.VMEM((own // 64, 128, 128), F32),
        ],
        compiler_params=pltpu.CompilerParams(vmem_limit_bytes=48 << 20),
        cost_estimate=pl.CostEstimate(
            flops=12 * 12 * rows * feats * own * 2, bytes_accessed=4 << 20, transcendentals=0
        ),
        name="sweep",
    )(core, states, initial, sizes, bias_out, in_own, out_own, bias_own, other)


def per_device(states, cotangent, obs_count, step_index, step_table, w_in, b_hid, w_out, b_out):
    rows = states.shape[0]
    local_seqs = obs_count.shape[0]
    slot_count = rows // local_seqs
    live = (jnp.arange(slot_count, dtype=jnp.int32)[None, :] < obs_count[:, None]).reshape(rows)
    initial = cotangent * live[:, None].astype(jnp.float32)
    table_ids = jnp.arange(step_table.shape[0], dtype=jnp.int32)

    def lookup(indices):
        picked = jnp.where(indices[:, None] == table_ids[None, :], step_table[None, :], 0.0)
        return jnp.sum(picked, axis=1)[None, :]

    sizes = jnp.stack([lookup(step_index[0]), lookup(step_index[1])])
    core = lax.axis_index("core")
    feats, own = w_in.shape
    bias = jnp.broadcast_to(b_hid[None, :], (8, own))
    mine = jnp.concatenate([jnp.where(core == 0, w_in, w_out), bias], axis=0)
    other = lax.all_gather(swapped(mine, "par"), "core")
    bias_out = jnp.broadcast_to(b_out[:, None], (feats, rows))
    back, keep, send = run_sweep(
        core.reshape(1), states, initial, sizes, bias_out, w_in, w_out, bias, other
    )
    keep, send = (v.reshape(feats // 2, 2 * own // 128, 128) for v in (keep, send))
    pair = (keep + swapped(send, "core")).astype(BF16)
    arrived = lax.all_to_all(pair, ("y", "z", "x"), split_axis=0, concat_axis=0, tiled=True)
    total = arrived.astype(F32).sum(axis=0).reshape(2, 1, own)
    return (back, total[0], total[1])


def solution(mesh):
    fine = Mesh(mesh.devices.reshape(SIZES), PLACE)
    return jax.shard_map(
        per_device,
        mesh=fine,
        in_specs=(
            P(SEQ, None),
            P(SEQ, None),
            P(SEQ),
            P(None, SEQ),
            P(),
            P(None, "par"),
            P("par"),
            P(None, "par"),
            P(),
        ),
        out_specs=(P(SEQ, None), P(SEQ, "par"), P(SEQ, "par")),
        check_vma=False,
    )
```

time: 79.7 us -> 72.1 us (0.905)
  matrix products: 29.9 us -> 0 us
  blocking collectives: 3.66 us -> 28.8 us
  Pallas kernels: 0 us -> 23.1 us
  starting transfers between devices: 22 us -> 8.13 us
  waiting for transfers between devices: 15.5 us -> 7.54 us
  other arithmetic: 3.6 us -> 1.41 us
  local copies, waits for them, and re-layouts: 3.43 us -> 2.17 us
    dot_general x71 -> x0, matrix products: 29.9 us -> none  [the longest x12 7.73 us: sweep(): jnp.einsum('rh,lh->rl', inner_b, w_in, preferred_element_type=jnp.float32)]
    all_to_all x0 -> x1, blocking collectives: none -> 25 us  [per_device(): lax.all_to_all(pair, ('y', 'z', 'x'), split_axis=0, concat_axis=0, tiled=...]
    pallas_call x0 -> x1, Pallas kernels: none -> 23.1 us  [run_sweep(): pl.pallas_call(sweep_kernel, out_shape=(jax.ShapeDtypeStruct((rows, feats...]
    all_to_all x1 -> x0, starting transfers between devices: 13.9 us -> none  [per_device(): lax.all_to_all(pair, ('y', 'z', 'x'), split_axis=0, concat_axis=0, tiled=...]
    all_to_all x1 -> x0, waiting for transfers between devices: 9.12 us -> none  [per_device(): lax.all_to_all(pair, ('y', 'z', 'x'), split_axis=0, concat_axis=0, tiled=...]
    ppermute x2, waiting for transfers between devices: 6.43 us -> 7.54 us  [swapped(): return lax.ppermute(value, PLACE, pairs)]
    unnamed x17 -> x18, local copies, waits for them, and re-layouts: 0.48 us -> 1.49 us
    squeeze x2 -> x0, local copies, waits for them, and re-layouts: 0.87 us -> none  [the longest x1 0.84 us: per_device(): send = lax.dynamic_index_in_dim(both, 1 - core, 1, keepdims=False)]
  transfers between devices with their start and end apart: 3 -> 2, of which waited for: 3 -> 2; matrix products, arithmetic and copies ran while one was open for 6% -> 0% of each run, Pallas kernels for 0% -> 0%
where the time goes in v2:
time: 72.1 us; the launch traced here: 71.9 us
  blocking collectives  28.8 us (40%)
  Pallas kernels  23.1 us (32%)
  starting transfers between devices  8.13 us (11%)
  waiting for transfers between devices  7.54 us (10%)
  local copies, waits for them, and re-layouts  2.17 us (3%)
  other arithmetic  1.41 us (2%)
  between operations  0.76 us (1%)
    all_to_all x1, blocking collectives, per_device(): lax.all_to_all(pair, ('y', 'z', 'x'), split_axis=0, concat_axis=0, tiled=...  25 us
    pallas_call x1, Pallas kernels, run_sweep(): pl.pallas_call(sweep_kernel, out_shape=(jax.ShapeDtypeStruct((rows, feats...  23.1 us
    ppermute x2, starting transfers between devices, swapped(): return lax.ppermute(value, PLACE, pairs)  8.13 us
    ppermute x2, waiting for transfers between devices, swapped(): return lax.ppermute(value, PLACE, pairs)  7.54 us
    all_gather x1, blocking collectives, per_device(): other = lax.all_gather(swapped(mine, 'par'), 'core')  3.79 us
    unnamed x18, local copies, waits for them, and re-layouts  1.49 us
  transfers between devices with their start and end apart: 2, of which 2 were waited for; matrix products, arithmetic and copies ran while one was open for 0% of the time, Pallas kernels for 0%

profile of v2, /device:TPU:1, one launch (start us, length us, event | category | flops | bytes accessed | tf_op | source)
XLA Modules:
  0.0 71.9 jit_solution(1097368833642257242)
XLA Ops:
  0.6 0.0 copy-start.4
  0.6 1.0 %broadcast_select_fusion = bf16[128,1024]{1,0:T(8,128)(2,1)S(1)} fusion(bf16[128,1024]{1,0:T(8,128)(2,1)} %in_own.1, bf16[128,1024]{1,0:T(8,128)(2,1)} %out_own.1, pred[]{:T(512)S(6)} %eq.41), kind=kLoop, calls=%fused_computation.3 | loop fusion | flops 131072 | bytes 786433 | tf_op jit(solution)/shard_map/jit(_where)/select_n | solution.py:199
  1.7 0.0 copy-start.8
  1.7 0.0 copy-start.5
  1.7 0.0 copy-start.3
  1.7 7.8 %collective-permute-start = (bf16[136,1024]{1,0:T(8,128)(2,1)S(1)}, bf16[136,1024]{1,0:T(8,128)(2,1)S(1)}, u32[]{:S(2)}, u32[]{:S(2)}) collective-permute-start(bf16[136,1024]{1,0:T(8,128)(2,1)S(1)} %pad_maximum_fusion), channel_id=1, source_target_pairs={{0,1},{1,0},{2,3},{3,2},{4,5},{5,4},{6,7},{7,6},{8,9},{9,8},{10,11... | collective-permute-start | bytes 835592 | tf_op jit(solution)/shard_map/ppermute | solution.py:22
  9.5 0.0 copy-done.8
  9.5 0.1 fusion
  9.6 0.7 copy-done.7
  10.3 0.1 select_reduce_fusion.1
  10.4 0.1 broadcast_multiply_fusion.initial
  10.5 0.0 copy-start
  10.5 0.0 copy-start.1
  10.5 5.9 %collective-permute-done = bf16[136,1024]{1,0:T(8,128)(2,1)S(1)} collective-permute-done((bf16[136,1024]{1,0:T(8,128)(2,1)S(1)}, bf16[136,1024]{1,0:T(8,128)(2,1)S(1)}, u32[]{:S(2)}, u32[]{:S(2)}) %collective-permute-start) | collective-permute-done | bytes 278560 | tf_op jit(solution)/shard_map/ppermute | solution.py:22
  16.5 3.8 %all-gather = bf16[272,1024]{1,0:T(8,128)(2,1)S(1)} all-gather(bf16[136,1024]{1,0:T(8,128)(2,1)S(1)} %collective-permute-done), channel_id=2, replica_groups=mesh['y'=4,'z'=4,'x'=4,'core'=2,'par'=2] {'core'}, dimensions={0}, use_global_device_ids=true | all-gather | bytes 835584 | tf_op jit(solution)/shard_map/all_gather | solution.py:200
  20.2 0.1 broadcast_in_dim.36.bias_out
  20.4 0.8 %copy-done.2 = f32[256,128]{1,0:T(8,128)S(1)} copy-done((f32[256,128]{1,0:T(8,128)S(1)}, f32[256,128]{1,0:T(8,128)}, u32[]{:S(2)}) %copy-start.2) | copy-done | bytes 131096
  21.1 23.1 %sweep.1 = (f32[256,128]{1,0:T(8,128)}, f32[1024,128]{1,0:T(8,128)S(1)}, f32[1024,128]{1,0:T(8,128)S(1)}) custom-call(s32[1]{0:T(128)} %bitcast.core, f32[256,128]{1,0:T(8,128)S(1)} %copy-done.2, f32[256,128]{1,0:T(8,128)S(1)} %broadcast_multiply_fusion.initial, f32[2,1,256]{2,1,0:T(1,128)S(1)} %pad_maximum_fusion.1.sizes, ...), custom_call_target="tpu_custom_call" | custom-call | flops 9663676416 | bytes 4194304 | tf_op jit(solution)/shard_map/sweep/pallas_call | solution.py:154
  44.3 0.3 collective-permute-start.1
  44.6 1.6 %collective-permute-done.1 = f32[64,16,128]{2,1,0:T(8,128)S(1)} collective-permute-done((f32[64,16,128]{2,1,0:T(8,128)S(1)}, f32[64,16,128]{2,1,0:T(8,128)S(1)}, u32[]{:S(2)}, u32[]{:S(2)}) %collective-permute-start.1) | collective-permute-done | bytes 524320 | tf_op jit(solution)/shard_map/ppermute | solution.py:22
  46.2 0.1 add_convert_fusion
  46.3 25.0 %all_to_all.5 = bf16[64,16,128]{2,1,0:T(8,128)(2,1)S(1)} all-to-all(bf16[64,16,128]{2,1,0:T(8,128)(2,1)S(1)} %add_convert_fusion), channel_id=1, replica_groups=mesh['y'=4,'z'=4,'x'=4,'core'=2,'par'=2] {'y','z','x'}, dimensions={0} | all-to-all | bytes 524288 | tf_op jit(solution)/shard_map/all_to_all | solution.py:207
  71.3 0.1 convert_reduce_fusion
  71.3 0.6 fusion.1
  (13 shorter events, 0.1 us)
Async XLA Ops:
  0.6 1.0 %copy-start.4 = (bf16[1024]{0:T(1024)(128)(2,1)S(1)}, bf16[1024]{0:T(1024)(128)(2,1)}, u32[]{:S(2)}) copy-start(bf16[1024]{0:T(1024)(128)(2,1)} %param.15) | copy-start | bytes 6148
  1.7 7.9 %copy-start.8 = (s32[2]{0:T(128)S(1)}, s32[2]{0:T(128)}, u32[]{:S(2)}) copy-start(s32[2]{0:T(128)} %param.11) | copy-start | bytes 28
  1.7 7.9 %copy-start.5 = (s32[2,256]{1,0:T(2,128)S(1)}, s32[2,256]{1,0:T(2,128)}, u32[]{:S(2)}) copy-start(s32[2,256]{1,0:T(2,128)} %param.12) | copy-start | bytes 6148
  1.7 8.7 %copy-start.3 = (f32[256,128]{1,0:T(8,128)S(1)}, f32[256,128]{1,0:T(8,128)}, u32[]{:S(2)}) copy-start(f32[256,128]{1,0:T(8,128)} %param.10) | copy-start | bytes 393220
  1.7 14.7 %collective-permute-start = (bf16[136,1024]{1,0:T(8,128)(2,1)S(1)}, bf16[136,1024]{1,0:T(8,128)(2,1)S(1)}, u32[]{:S(2)}, u32[]{:S(2)}) collective-permute-start(bf16[136,1024]{1,0:T(8,128)(2,1)S(1)} %pad_maximum_fusion), channel_id=1, source_target_pairs={{0,1},{1,0},{2,3},{3,2},{4,5},{5,4},{6,7},{7,6},{8,9},{9,8},{10,11... | collective-permute-start | bytes 835592 | tf_op jit(solution)/shard_map/ppermute | solution.py:22
  9.6 0.7 copy-start.7
  10.5 9.9 %copy-start = (bf16[128,1024]{1,0:T(8,128)(2,1)S(1)}, bf16[128,1024]{1,0:T(8,128)(2,1)}, u32[]{:S(2)}) copy-start(bf16[128,1024]{1,0:T(8,128)(2,1)} %in_own.1) | copy-start | bytes 786436
  10.5 9.9 %copy-start.1 = (bf16[128,1024]{1,0:T(8,128)(2,1)S(1)}, bf16[128,1024]{1,0:T(8,128)(2,1)}, u32[]{:S(2)}) copy-start(bf16[128,1024]{1,0:T(8,128)(2,1)} %out_own.1) | copy-start | bytes 786436
  16.4 3.8 %copy-start.6 = (f32[128]{0:T(128)S(1)}, f32[128]{0:T(128)}, u32[]{:S(2)}) copy-start(f32[128]{0:T(128)} %param.17) | copy-start | bytes 1540
  20.2 0.9 %copy-start.2 = (f32[256,128]{1,0:T(8,128)S(1)}, f32[256,128]{1,0:T(8,128)}, u32[]{:S(2)}) copy-start(f32[256,128]{1,0:T(8,128)} %states.1) | copy-start | bytes 393220
  44.3 1.9 %collective-permute-start.1 = (f32[64,16,128]{2,1,0:T(8,128)S(1)}, f32[64,16,128]{2,1,0:T(8,128)S(1)}, u32[]{:S(2)}, u32[]{:S(2)}) collective-permute-start(f32[64,16,128]{2,1,0:T(8,128)S(1)} %bitcast.14), channel_id=1, source_target_pairs={{0,2},{1,3},{2,0},{3,1},{4,6},{5,7},{6,4},{7,5},{8,10},{9,11},{10,... | collective-permute-start | bytes 1572872 | tf_op jit(solution)/shard_map/ppermute | solution.py:22

commit v3 on v2

--- a/solution.py
+++ b/solution.py
@@ -17,9 +17,10 @@
     pairs = []
     for source in range(int(np.prod(SIZES))):
         place = list(np.unravel_index(source, SIZES))
-        place[at] = 1 - place[at]
+        place[at] ^= 1
         pairs.append((source, int(np.ravel_multi_index(place, SIZES))))
     return lax.ppermute(value, PLACE, pairs)
+
 
 COEF_A = [
     [],
@@ -50,30 +51,64 @@
     )
 
 
+def turn_weights(w_in, w_out, bias, in_t, out_t, start):
+    feats, units = w_in.shape
+    for at in range(0, units, 128):
+        to = pl.ds(start + at, 128)
+        in_t[to, :feats] = w_in[:, at : at + 128].T
+        low = jnp.concatenate(
+            [bias[:, at : at + 128].astype(F32), jnp.zeros((128 - bias.shape[0], 128), F32)]
+        )
+        in_t[to, feats:] = low.T.astype(BF16)
+        out_t[to, :] = w_out[:, at : at + 128].T
+
+
+def prepare_kernel(states, initial, w_in, w_out, bias, states_t, initial_t, in_t, out_t):
+    states_t[...] = transposed(states[...])
+    initial_t[...] = transposed(initial[...])
+    turn_weights(w_in, w_out, bias, in_t, out_t, 0)
+
+
+def prepare(states, initial, w_in, w_out, bias):
+    rows, feats = states.shape
+    own = w_in.shape[1]
+    space = pl.BlockSpec(memory_space=pltpu.VMEM)
+    return pl.pallas_call(
+        prepare_kernel,
+        out_shape=(
+            jax.ShapeDtypeStruct((feats, rows), F32),
+            jax.ShapeDtypeStruct((feats, rows), F32),
+            jax.ShapeDtypeStruct((own, 2 * feats), BF16),
+            jax.ShapeDtypeStruct((own, feats), BF16),
+        ),
+        in_specs=[space] * 5,
+        out_specs=(space,) * 4,
+        compiler_params=pltpu.CompilerParams(vmem_limit_bytes=8 << 20),
+        cost_estimate=pl.CostEstimate(flops=200_000_000, bytes_accessed=2 << 20, transcendentals=0),
+        name="prepare",
+    )(states, initial, w_in, w_out, bias)
+
+
 def sweep_kernel(
-    core, states, initial, sizes, bias_out, in_own, out_own, bias_own, other,
+    core, states_t, initial_t, in_t_own, out_t_own, sizes, bias_out, in_own, out_own, near, far,
     back, keep, send,
-    in_t, out_t, hid, slope_of, probe, value, terms, acc_in, acc_out, square,
+    in_t_other, out_t_other, hid, slope_of, probe, value, terms, acc_in, acc_out, square,
 ):
     feats, own = in_own.shape
-    rows = states.shape[0]
-    in_other, out_other, bias_other = other.at[0, :feats], other.at[1, :feats], other.at[0, feats:]
-    for half, (w_in, w_out, bias) in enumerate(
-        ((in_own, out_own, bias_own), (in_other, out_other, bias_other))
-    ):
-        for at in range(0, own, 128):
-            to = pl.ds(half * own + at, 128)
-            in_t[to, :feats] = w_in[:, at : at + 128].T
-            low = jnp.concatenate(
-                [bias[:, at : at + 128].astype(F32), jnp.zeros((128 - bias.shape[0], 128), F32)]
-            )
-            in_t[to, feats:] = low.T.astype(BF16)
-            out_t[to, :] = w_out[:, at : at + 128].T
-    value[...] = transposed(states[...])
+    rows = states_t.shape[1]
+    part = near.shape[2]
+    for start, got in ((0, near), (part, far)):
+        turn_weights(
+            got.at[0, :feats], got.at[1, :feats], got.at[0, feats:], in_t_other, out_t_other, start
+        )
+    value[...] = states_t[...]
     acc_in[...] = jnp.zeros_like(acc_in)
     acc_out[...] = jnp.zeros_like(acc_out)
     unit = jnp.where(lax.broadcasted_iota(jnp.int32, (feats, rows), 0) == 0, 1.0, 0.0).astype(BF16)
     bias_o = bias_out[...]
+
+    def rows_of(first, second, at):
+        return first[at : at + BLOCK] if at < own else second[at - own : at - own + BLOCK]
 
     def forward(step, _):
         size = sizes[step]
@@ -88,12 +123,13 @@
             probe[step, now] = state_b
             full = jnp.concatenate([state_b, unit], axis=0)
             for at in range(0, 2 * own, BLOCK):
-                hidden = jnp.tanh(dot(in_t[at : at + BLOCK], full))
+                hidden = jnp.tanh(dot(rows_of(in_t_own, in_t_other, at), full))
                 hid[step, now, at : at + BLOCK] = hidden.astype(BF16)
                 slope_of[step, now, at : at + BLOCK] = (1.0 - hidden * hidden).astype(BF16)
             terms[now] = (
                 dot(out_own[...], hid[step, now, :own])
-                + dot(out_other[...], hid[step, now, own:])
+                + dot(near[1, :feats], hid[step, now, own : own + part])
+                + dot(far[1, :feats], hid[step, now, own + part :])
                 + bias_o
             )
         combo = COEF_B[0] * terms[0]
@@ -103,7 +139,7 @@
         return 0
 
     lax.fori_loop(0, 2, forward, 0)
-    value[...] = transposed(initial[...])
+    value[...] = initial_t[...]
 
     def backward(turn, _):
         step = 1 - turn
@@ -114,12 +150,14 @@
                 combo = combo + COEF_A[later][now] * terms[later]
             grad_b = (size * combo).astype(BF16)
             for at in range(0, 2 * own, BLOCK):
-                inner = dot(out_t[at : at + BLOCK], grad_b) * slope_of[
+                inner = dot(rows_of(out_t_own, out_t_other, at), grad_b) * slope_of[
                     step, now, at : at + BLOCK
                 ].astype(F32)
                 slope_of[step, now, at : at + BLOCK] = inner.astype(BF16)
-            terms[now] = dot(in_own[...], slope_of[step, now, :own]) + dot(
-                in_other[...], slope_of[step, now, own:]
+            terms[now] = (
+                dot(in_own[...], slope_of[step, now, :own])
+                + dot(near[0, :feats], slope_of[step, now, own : own + part])
+                + dot(far[0, :feats], slope_of[step, now, own + part :])
             )
             acc_in[...] += dot(slope_of[step, now, :own], probe[step, now], (1, 1))
             acc_out[...] += dot(hid[step, now, :own], grad_b, (1, 1))
@@ -146,8 +184,8 @@
                 send[line, :] = square[at, pl.ds(1 - side, feats // 2, stride=2), :]
 
 
-def run_sweep(core, states, initial, sizes, bias_out, in_own, out_own, bias_own, other):
-    rows, feats = states.shape
+def run_sweep(core, prepared, sizes, bias_out, in_own, out_own, near, far):
+    feats, rows = prepared[0].shape
     own = in_own.shape[1]
     lines = feats * own // 128
     space = pl.BlockSpec(memory_space=pltpu.VMEM)
@@ -158,11 +196,11 @@
             jax.ShapeDtypeStruct((lines, 128), F32),
             jax.ShapeDtypeStruct((lines, 128), F32),
         ),
-        in_specs=[pl.BlockSpec(memory_space=pltpu.SMEM)] + [space] * 8,
+        in_specs=[pl.BlockSpec(memory_space=pltpu.SMEM)] + [space] * 10,
         out_specs=(space,) * 3,
         scratch_shapes=[
-            pltpu.VMEM((2 * own, 2 * feats), BF16),
-            pltpu.VMEM((2 * own, feats), BF16),
+            pltpu.VMEM((own, 2 * feats), BF16),
+            pltpu.VMEM((own, feats), BF16),
             pltpu.VMEM((2, 6, 2 * own, rows), BF16),
             pltpu.VMEM((2, 6, 2 * own, rows), BF16),
             pltpu.VMEM((2, 6, feats, rows), BF16),
@@ -177,7 +215,7 @@
             flops=12 * 12 * rows * feats * own * 2, bytes_accessed=4 << 20, transcendentals=0
         ),
         name="sweep",
-    )(core, states, initial, sizes, bias_out, in_own, out_own, bias_own, other)
+    )(core, *prepared, sizes, bias_out, in_own, out_own, near, far)
 
 
 def per_device(states, cotangent, obs_count, step_index, step_table, w_in, b_hid, w_out, b_out):
@@ -195,12 +233,18 @@
     sizes = jnp.stack([lookup(step_index[0]), lookup(step_index[1])])
     core = lax.axis_index("core")
     feats, own = w_in.shape
+    part = own // 2
     bias = jnp.broadcast_to(b_hid[None, :], (8, own))
-    mine = jnp.concatenate([jnp.where(core == 0, w_in, w_out), bias], axis=0)
-    other = lax.all_gather(swapped(mine, "par"), "core")
+    odd = lax.axis_index("x") % 2
+    layer = jnp.concatenate([jnp.where(core == 0, w_in, w_out), bias], axis=0)
+    piece = jnp.where(odd == 0, layer[:, :part], layer[:, part:])
+    near = swapped(piece, "par")
+    far = swapped(near, "x")
+    near, far = lax.all_gather(near, "core"), lax.all_gather(far, "core")
     bias_out = jnp.broadcast_to(b_out[:, None], (feats, rows))
+    prepared = prepare(states, initial, w_in, w_out, bias)
     back, keep, send = run_sweep(
-        core.reshape(1), states, initial, sizes, bias_out, w_in, w_out, bias, other
+        core.reshape(1), prepared, sizes, bias_out, w_in, w_out, near, far
     )
     keep, send = (v.reshape(feats // 2, 2 * own // 128, 128) for v in (keep, send))
     pair = (keep + swapped(send, "core")).astype(BF16)

time: 72.1 us -> 70.3 us (0.975)
  waiting for transfers between devices: 7.54 us -> 2.43 us
  starting transfers between devices: 8.13 us -> 9.78 us
  blocking collectives: 28.8 us -> 29.8 us
    ppermute x2 -> x3, waiting for transfers between devices: 7.54 us -> 2.43 us  [swapped(): return lax.ppermute(value, PLACE, pairs)]
    all_gather x1 -> x2, blocking collectives: 3.79 us -> 6.81 us  [per_device(): near, far = (lax.all_gather(near, 'core'), lax.all_gather(far, 'core'))]
    all_to_all x1, blocking collectives: 25 us -> 23 us  [per_device(): lax.all_to_all(pair, ('y', 'z', 'x'), split_axis=0, concat_axis=0, tiled=...]
    ppermute x2 -> x3, starting transfers between devices: 8.13 us -> 9.78 us  [swapped(): return lax.ppermute(value, PLACE, pairs)]
  transfers between devices with their start and end apart: 2 -> 3, of which waited for: 2 -> 2; matrix products, arithmetic and copies ran while one was open for 0% -> 0% of each run, Pallas kernels for 0% -> 1%
where the time goes in v3:
time: 70.3 us; the launch traced here: 70.1 us
  blocking collectives  29.8 us (42%)
  Pallas kernels  23 us (33%)
  starting transfers between devices  9.78 us (14%)
  local copies, waits for them, and re-layouts  2.82 us (4%)
  waiting for transfers between devices  2.43 us (3%)
  other arithmetic  1.47 us (2%)
  between operations  0.76 us (1%)
    all_to_all x1, blocking collectives, per_device(): lax.all_to_all(pair, ('y', 'z', 'x'), split_axis=0, concat_axis=0, tiled=...  23 us
    pallas_call x1, Pallas kernels, run_sweep(): pl.pallas_call(sweep_kernel, out_shape=(jax.ShapeDtypeStruct((rows, feats...  22.6 us
    ppermute x3, starting transfers between devices, swapped(): return lax.ppermute(value, PLACE, pairs)  9.78 us
    all_gather x2, blocking collectives, per_device(): near, far = (lax.all_gather(near, 'core'), lax.all_gather(far, 'core'))  6.81 us
    ppermute x3, waiting for transfers between devices, swapped(): return lax.ppermute(value, PLACE, pairs)  2.43 us
    unnamed x18, local copies, waits for them, and re-layouts  2.14 us
  transfers between devices with their start and end apart: 3, of which 2 were waited for; matrix products, arithmetic and copies ran while one was open for 0% of the time, Pallas kernels for 1%

profile of v3, /device:TPU:1, one launch (start us, length us, event | category | flops | bytes accessed | tf_op | source)
XLA Modules:
  0.0 70.1 jit_solution(1350418234266248524)
XLA Ops:
  0.7 1.0 %broadcast_select_fusion = bf16[128,1024]{1,0:T(8,128)(2,1)S(1)} fusion(bf16[128,1024]{1,0:T(8,128)(2,1)} %in_own.1, bf16[128,1024]{1,0:T(8,128)(2,1)} %out_own.1, pred[]{:T(512)S(6)} %eq.47), kind=kLoop, calls=%fused_computation.4 | loop fusion | flops 131072 | bytes 786433 | tf_op jit(solution)/shard_map/jit(_where)/select_n | solution.py:239
  1.8 0.0 copy-start.1
  1.8 7.8 %collective-permute-start = (bf16[136,512]{1,0:T(8,128)(2,1)S(1)}, bf16[136,512]{1,0:T(8,128)(2,1)S(1)}, u32[]{:S(2)}, u32[]{:S(2)}) collective-permute-start(bf16[136,512]{1,0:T(8,128)(2,1)S(1)} %fusion.1), channel_id=1, source_target_pairs={{0,1},{1,0},{2,3},{3,2},{4,5},{5,4},{6,7},{7,6},{8,9},{9,8},{10,11... | collective-permute-start | bytes 417800 | tf_op jit(solution)/shard_map/ppermute | solution.py:22
  9.6 0.1 fusion.2
  9.7 0.1 broadcast_multiply_fusion.initial
  9.8 0.6 copy-done.5
  10.4 0.2 copy-done.2
  10.6 0.4 prepare.1
  11.0 0.0 copy-start.7
  11.0 0.6 copy-done.7
  11.7 0.1 select_reduce_fusion.1
  11.7 0.8 %collective-permute-done = bf16[136,512]{1,0:T(8,128)(2,1)S(1)} collective-permute-done((bf16[136,512]{1,0:T(8,128)(2,1)S(1)}, bf16[136,512]{1,0:T(8,128)(2,1)S(1)}, u32[]{:S(2)}, u32[]{:S(2)}) %collective-permute-start) | collective-permute-done | bytes 139296 | tf_op jit(solution)/shard_map/ppermute | solution.py:22
  12.6 1.7 %collective-permute-start.1 = (bf16[136,512]{1,0:T(8,128)(2,1)S(1)}, bf16[136,512]{1,0:T(8,128)(2,1)S(1)}, u32[]{:S(2)}, u32[]{:S(2)}) collective-permute-start(bf16[136,512]{1,0:T(8,128)(2,1)S(1)} %collective-permute-done), channel_id=1, source_target_pairs={{0,4},{1,5},{2,6},{3,7},{4,0},{5,1},{6,2},{7,3},{8,12},{9,13},{10,... | collective-permute-start | bytes 417800 | tf_op jit(solution)/shard_map/ppermute | solution.py:22
  14.2 3.3 %all-gather = bf16[272,512]{1,0:T(8,128)(2,1)S(1)} all-gather(bf16[136,512]{1,0:T(8,128)(2,1)S(1)} %collective-permute-done), channel_id=2, replica_groups=mesh['y'=4,'z'=4,'x'=4,'core'=2,'par'=2] {'core'}, dimensions={0}, use_global_device_ids=true | all-gather | bytes 417792 | tf_op jit(solution)/shard_map/all_gather | solution.py:243
  17.5 3.6 %all-gather.1 = bf16[272,512]{1,0:T(8,128)(2,1)S(1)} all-gather(bf16[136,512]{1,0:T(8,128)(2,1)S(1)} %collective-permute-done.1), channel_id=3, replica_groups=mesh['y'=4,'z'=4,'x'=4,'core'=2,'par'=2] {'core'}, dimensions={0}, use_global_device_ids=true | all-gather | bytes 417792 | tf_op jit(solution)/shard_map/all_gather | solution.py:243
  21.0 0.7 copy-done.6
  21.7 0.1 broadcast_in_dim.37.bias_out
  21.8 22.6 %sweep.1 = (f32[256,128]{1,0:T(8,128)}, f32[1024,128]{1,0:T(8,128)S(1)}, f32[1024,128]{1,0:T(8,128)S(1)}) custom-call(s32[1]{0:T(128)} %bitcast.core, f32[128,256]{1,0:T(8,128)S(1)} %get-tuple-element.10.states_t, f32[128,256]{1,0:T(8,128)S(1)} %get-tuple-element.11.initial_t, bf16[1024,256]{1,0:T(8,128)(2,1)S(1)} %get-tuple-element.12.in_t_own, ...), custom_call_target="tpu_custom_call" | custom-call | flops 9663676416 | bytes 4194304 | tf_op jit(solution)/shard_map/sweep/pallas_call | solution.py:192
  44.4 0.3 collective-permute-start.2
  44.7 1.6 %collective-permute-done.2 = f32[64,16,128]{2,1,0:T(8,128)S(1)} collective-permute-done((f32[64,16,128]{2,1,0:T(8,128)S(1)}, f32[64,16,128]{2,1,0:T(8,128)S(1)}, u32[]{:S(2)}, u32[]{:S(2)}) %collective-permute-start.2) | collective-permute-done | bytes 524320 | tf_op jit(solution)/shard_map/ppermute | solution.py:22
  46.3 0.1 add_convert_fusion
  46.4 23.0 %all_to_all.5 = bf16[64,16,128]{2,1,0:T(8,128)(2,1)S(1)} all-to-all(bf16[64,16,128]{2,1,0:T(8,128)(2,1)S(1)} %add_convert_fusion), channel_id=1, replica_groups=mesh['y'=4,'z'=4,'x'=4,'core'=2,'par'=2] {'y','z','x'}, dimensions={0} | all-to-all | bytes 524288 | tf_op jit(solution)/shard_map/all_to_all | solution.py:251
  69.4 0.1 convert_reduce_fusion
  69.5 0.6 fusion.3
  (17 shorter events, 0.1 us)
Async XLA Ops:
  0.6 1.1 %copy-start.4 = (bf16[1024]{0:T(1024)(128)(2,1)S(1)}, bf16[1024]{0:T(1024)(128)(2,1)}, u32[]{:S(2)}) copy-start(bf16[1024]{0:T(1024)(128)(2,1)} %param.15) | copy-start | bytes 6148
  0.7 9.0 %copy-start.3 = (f32[256,128]{1,0:T(8,128)S(1)}, f32[256,128]{1,0:T(8,128)}, u32[]{:S(2)}) copy-start(f32[256,128]{1,0:T(8,128)} %param.10) | copy-start | bytes 393220
  1.7 7.9 %copy-start.8 = (s32[2]{0:T(128)S(1)}, s32[2]{0:T(128)}, u32[]{:S(2)}) copy-start(s32[2]{0:T(128)} %param.11) | copy-start | bytes 28
  1.7 8.6 %copy-start = (bf16[128,1024]{1,0:T(8,128)(2,1)S(1)}, bf16[128,1024]{1,0:T(8,128)(2,1)}, u32[]{:S(2)}) copy-start(bf16[128,1024]{1,0:T(8,128)(2,1)} %in_own.1) | copy-start | bytes 786436
  1.8 8.6 %copy-start.1 = (bf16[128,1024]{1,0:T(8,128)(2,1)S(1)}, bf16[128,1024]{1,0:T(8,128)(2,1)}, u32[]{:S(2)}) copy-start(bf16[128,1024]{1,0:T(8,128)(2,1)} %out_own.1) | copy-start | bytes 786436
  1.8 10.8 %collective-permute-start = (bf16[136,512]{1,0:T(8,128)(2,1)S(1)}, bf16[136,512]{1,0:T(8,128)(2,1)S(1)}, u32[]{:S(2)}, u32[]{:S(2)}) collective-permute-start(bf16[136,512]{1,0:T(8,128)(2,1)S(1)} %fusion.1), channel_id=1, source_target_pairs={{0,1},{1,0},{2,3},{3,2},{4,5},{5,4},{6,7},{7,6},{8,9},{9,8},{10,11... | collective-permute-start | bytes 417800 | tf_op jit(solution)/shard_map/ppermute | solution.py:22
  9.7 0.7 copy-start.5
  9.7 0.9 %copy-start.2 = (f32[256,128]{1,0:T(8,128)S(1)}, f32[256,128]{1,0:T(8,128)}, u32[]{:S(2)}) copy-start(f32[256,128]{1,0:T(8,128)} %states.1) | copy-start | bytes 393220
  11.0 0.7 copy-start.7
  12.6 4.9 %collective-permute-start.1 = (bf16[136,512]{1,0:T(8,128)(2,1)S(1)}, bf16[136,512]{1,0:T(8,128)(2,1)S(1)}, u32[]{:S(2)}, u32[]{:S(2)}) collective-permute-start(bf16[136,512]{1,0:T(8,128)(2,1)S(1)} %collective-permute-done), channel_id=1, source_target_pairs={{0,4},{1,5},{2,6},{3,7},{4,0},{5,1},{6,2},{7,3},{8,12},{9,13},{10,... | collective-permute-start | bytes 417800 | tf_op jit(solution)/shard_map/ppermute | solution.py:22
  21.0 0.7 copy-start.6
  44.4 1.9 %collective-permute-start.2 = (f32[64,16,128]{2,1,0:T(8,128)S(1)}, f32[64,16,128]{2,1,0:T(8,128)S(1)}, u32[]{:S(2)}, u32[]{:S(2)}) collective-permute-start(f32[64,16,128]{2,1,0:T(8,128)S(1)} %bitcast.16), channel_id=1, source_target_pairs={{0,2},{1,3},{2,0},{3,1},{4,6},{5,7},{6,4},{7,5},{8,10},{9,11},{10,... | collective-permute-start | bytes 1572872 | tf_op jit(solution)/shard_map/ppermute | solution.py:22

commit v4 on v3

v4 whole, which is shorter than its diff:
```python
import functools

import jax
import jax.numpy as jnp
import numpy as np
from jax import lax
from jax.experimental import pallas as pl
from jax.experimental.pallas import tpu as pltpu
from jax.sharding import Mesh
from jax.sharding import PartitionSpec as P

SEQ = ("y", "z", "x", "core")
PLACE = SEQ + ("par",)
SIZES = (4, 4, 4, 2, 2)


def swapped(value, axis):
    at = PLACE.index(axis)
    pairs = []
    for source in range(int(np.prod(SIZES))):
        place = list(np.unravel_index(source, SIZES))
        place[at] ^= 1
        pairs.append((source, int(np.ravel_multi_index(place, SIZES))))
    return lax.ppermute(value, PLACE, pairs)


COEF_A = [
    [],
    [1.0 / 5],
    [3.0 / 40, 9.0 / 40],
    [44.0 / 45, -56.0 / 15, 32.0 / 9],
    [19372.0 / 6561, -25360.0 / 2187, 64448.0 / 6561, -212.0 / 729],
    [9017.0 / 3168, -355.0 / 33, 46732.0 / 5247, 49.0 / 176, -5103.0 / 18656],
]
COEF_B = [35.0 / 384, 0.0, 500.0 / 1113, 125.0 / 192, -2187.0 / 6784, 11.0 / 84]
F32, BF16 = jnp.float32, jnp.bfloat16
TILE, PIECE = 256, 128
PIECES = 8


def transposed(value):
    rows, columns = value.shape
    return jnp.concatenate(
        [
            jnp.concatenate([value[i : i + 128, j : j + 128].T for i in range(0, rows, 128)], axis=1)
            for j in range(0, columns, 128)
        ],
        axis=0,
    )


def turned_in(square, bias):
    low = jnp.concatenate([bias.astype(F32), jnp.zeros((128 - bias.shape[0], 128), F32)])
    return jnp.concatenate([square.T, low.T.astype(BF16)], axis=1)


def turned_out(square):
    return jnp.concatenate([square.T, jnp.zeros((128, 128), BF16)], axis=1)


def prepare_kernel(
    counts, table, states, cotangent, index, w_in, w_out, bias, b_out,
    states_t, initial_t, sizes, in_t, out_t, bias_t,
):
    rows = states.shape[0]
    states_t[...] = transposed(states[...])
    slot = lax.broadcasted_iota(jnp.int32, (1, rows), 1)
    slots = rows // counts.shape[0]
    live = jnp.zeros((1, rows), F32)
    for which in range(counts.shape[0]):
        first = which * slots
        inside = (slot >= first) & (slot < first + counts[which])
        live = jnp.where(inside, 1.0, live)
    initial_t[...] = transposed(cotangent[...]) * live
    size = jnp.zeros(index.shape, F32)
    for entry in range(table.shape[0]):
        size = jnp.where(index[...] == entry, table[entry], size)
    sizes[...] = size
    column = jnp.broadcast_to(b_out[...], (128, 128)).T
    bias_t[...] = jnp.concatenate([column, column], axis=1)
    for at in range(0, w_in.shape[1], 128):
        here = slice(at, at + 128)
        in_t[here] = turned_in(w_in[:, here], bias[:, here])
        out_t[here] = turned_out(w_out[:, here])


def prepare(counts, table, states, cotangent, index, w_in, w_out, bias, b_out):
    rows, feats = states.shape
    own = w_in.shape[1]
    space = pl.BlockSpec(memory_space=pltpu.VMEM)
    return pl.pallas_call(
        prepare_kernel,
        out_shape=(
            jax.ShapeDtypeStruct((feats, rows), F32),
            jax.ShapeDtypeStruct((feats, rows), F32),
            jax.ShapeDtypeStruct(index.shape, F32),
            jax.ShapeDtypeStruct((own, 2 * feats), BF16),
            jax.ShapeDtypeStruct((own, 2 * feats), BF16),
            jax.ShapeDtypeStruct((feats, rows), F32),
        ),
        in_specs=[pl.BlockSpec(memory_space=pltpu.SMEM)] * 2 + [space] * 7,
        out_specs=(space,) * 6,
        compiler_params=pltpu.CompilerParams(vmem_limit_bytes=8 << 20),
        cost_estimate=pl.CostEstimate(flops=200_000_000, bytes_accessed=2 << 20, transcendentals=0),
        name="prepare",
    )(counts, table, states, cotangent, index, w_in, w_out, bias, b_out)


def sweep_kernel(
    core, states_t, initial_t, sizes, in_t_own, out_t_own, bias_t, in_own, out_own,
    near, near_peer, far, far_peer,
    back, keep, send,
    in_t_other, out_t_other, in_other, out_other, hid, hid_own, inner_own, probe, value, terms, grads,
    *accumulators,
):
    feats, own = in_own.shape
    rows = states_t.shape[1]
    part = near.shape[1]
    tiles = 2 * own // TILE
    first_core = core[0] == 0
    for start, mine, peer in ((0, near, near_peer), (part, far, far_peer)):
        for at in range(0, part, 128):
            here, to = slice(at, at + 128), slice(start + at, start + at + 128)
            a, b = mine[:feats, here], peer[:feats, here]
            square_in, square_out = jnp.where(first_core, a, b), jnp.where(first_core, b, a)
            in_other[:, to] = square_in
            out_other[:, to] = square_out
            in_t_other[to] = turned_in(square_in, mine[feats:, here])
            out_t_other[to] = turned_out(square_out)
    grads[...] = jnp.zeros_like(grads)
    unit = jnp.where(lax.broadcasted_iota(jnp.int32, (feats, rows), 0) == 0, 1.0, 0.0).astype(BF16)
    nothing = jnp.zeros((feats, rows), BF16)
    held = [accumulators[:PIECES], accumulators[PIECES:]]
    turns = [0, 0]

    def push(q, tile, transpose=False):
        register = turns[q] % 2
        turns[q] += 1
        pltpu.matmul_push_rhs(tile, staging_register=register, mxu_index=q, transpose=transpose)
        return register

    def place(q, number):
        return (2 * number + q) * TILE

    def lines(first, second, at, count):
        return first[at : at + count] if at < own else second[at - own : at - own + count]

    def columns(first, second, at):
        return first[:, at : at + TILE] if at < own else second[:, at - own : at - own + TILE]

    def slot(q, piece):
        return held[q][piece % 7]

    def stream(weights, q, piece, register):
        at = place(q, piece // 2) + piece % 2 * PIECE
        pltpu.matmul_acc_lhs(
            slot(q, piece), lines(*weights, at, PIECE), load_staged_rhs=register
        )

    def forward(step, _):
        size = sizes[pl.ds(step, 1), :]
        for now in range(6):
            state = value[...]
            if now > 1:
                combo = COEF_A[now][0] * terms[0]
                for before in range(1, now - 1):
                    combo = combo + COEF_A[now][before] * terms[before]
                state = state + size * combo
            if now:
                state = state + (COEF_A[now][now - 1] * size) * terms[now - 1]
            state_b = state.astype(BF16)
            probe[step, now] = state_b
            full = jnp.concatenate([state_b, unit], axis=0)
            staged = [push(q, full) for q in range(2)]
            for piece in range(7):
                for q in range(2):
                    stream((in_t_own, in_t_other), q, piece, None if piece else staged[q])
            for number in range(4):
                ready = [[], []]
                for half in range(2):
                    for q in range(2):
                        piece = 2 * number + half
                        hidden = jnp.tanh(pltpu.matmul_pop(slot(q, piece)))
                        if piece == 0:
                            stream((in_t_own, in_t_other), q, 7, None)
                        hidden_b = hidden.astype(BF16)
                        at = place(q, number) + half * PIECE
                        hid[step, now, at : at + PIECE] = hidden
                        if number < 2:
                            hid_own[step, now, at : at + PIECE] = hidden_b
                        ready[q].append(hidden_b)
                for q in range(2):
                    register = push(q, jnp.concatenate(ready[q], axis=0))
                    pltpu.matmul_acc_lhs(
                        held[q][7],
                        columns(out_own, out_other, place(q, number)),
                        load_staged_rhs=register,
                    )
            terms[now] = pltpu.matmul_pop(held[0][7]) + pltpu.matmul_pop(held[1][7]) + bias_t[...]
        combo = COEF_B[0] * terms[0]
        for now in range(2, 6):
            combo = combo + COEF_B[now] * terms[now]
        value[...] = value[...] + size * combo
        return 0

    def collect(q, which, number):
        product = pltpu.matmul_pop(held[q][(1 if which else 3) + number])
        for half in range(2):
            at = which * (own // 128) + 2 * (2 * number + q) + half
            grads[at] += product[:, half * 128 : (half + 1) * 128]

    def backward(turn, _):
        step = 1 - turn
        size = sizes[pl.ds(step, 1), :]
        for now in reversed(range(6)):
            combo = COEF_B[now] * value[...]
            for later in range(5, now + 1, -1):
                combo = combo + COEF_A[later][now] * terms[later]
            combo = size * combo
            if now < 5:
                combo = combo + (COEF_A[now + 1][now] * size) * terms[now + 1]
            grad_b = combo.astype(BF16)
            full = jnp.concatenate([grad_b, nothing], axis=0)
            staged = [push(q, full) for q in range(2)]
            for piece in range(3):
                for q in range(2):
                    stream((out_t_own, out_t_other), q, piece, None if piece else staged[q])
            if now < 5:
                for number in range(2):
                    for q in range(2):
                        collect(q, 0, number)
            for piece in range(3, 7):
                for q in range(2):
                    stream((out_t_own, out_t_other), q, piece, None)
            late = []
            for number in range(2):
                for q in range(2):
                    at = place(q, number)
                    late.append(push(q, hid_own[step, now, at : at + TILE], transpose=True))
            for number in range(4):
                ready = [[], []]
                for half in range(2):
                    for q in range(2):
                        piece = 2 * number + half
                        at = place(q, number) + half * PIECE
                        hidden = hid[step, now, at : at + PIECE]
                        inner = pltpu.matmul_pop(slot(q, piece)) * (1.0 - hidden * hidden)
                        if piece == 0:
                            stream((out_t_own, out_t_other), q, 7, None)
                        inner_b = inner.astype(BF16)
                        if number < 2:
                            inner_own[at : at + PIECE] = inner_b
                        ready[q].append(inner_b)
                if number < 2:
                    for q in range(2):
                        pltpu.matmul_acc_lhs(
                            held[q][1 + number], grad_b, load_staged_rhs=late[2 * number + q]
                        )
                for q in range(2):
                    register = push(q, jnp.concatenate(ready[q], axis=0))
                    pltpu.matmul_acc_lhs(
                        held[q][7],
                        columns(in_own, in_other, place(q, number)),
                        load_staged_rhs=register,
                    )
            for number in range(2):
                for q in range(2):
                    at = place(q, number)
                    register = push(q, inner_own[at : at + TILE], transpose=True)
                    pltpu.matmul_acc_lhs(
                        held[q][3 + number], probe[step, now], load_staged_rhs=register
                    )
            for number in range(2):
                for q in range(2):
                    collect(q, 1, number)
            terms[now] = pltpu.matmul_pop(held[0][7]) + pltpu.matmul_pop(held[1][7])
        for number in range(2):
            for q in range(2):
                collect(q, 0, number)
        total = value[...]
        for now in reversed(range(6)):
            total = total + terms[now]
        value[...] = total
        return 0

    value[...] = states_t[...]
    lax.fori_loop(0, 2, forward, 0)
    value[...] = initial_t[...]
    lax.fori_loop(0, 2, backward, 0)
    back[...] = transposed(value[...])
    width = 2 * own // 128
    for side in range(2):

        @pl.when(core[0] == side)
        def _():
            for at in range(width):
                line = pl.ds(at, feats // 2, stride=width)
                keep[line, :] = grads[at, pl.ds(side, feats // 2, stride=2), :]
                send[line, :] = grads[at, pl.ds(1 - side, feats // 2, stride=2), :]


def scoped(count, *refs):
    specs = [pltpu.ACC(q)((PIECE, TILE), F32) for q in range(2) for _ in range(PIECES)]
    pl.run_scoped(lambda *accumulators: sweep_kernel(*refs, *accumulators), *specs)


def run_sweep(core, prepared, in_own, out_own, pieces):
    feats, rows = prepared[0].shape
    own = in_own.shape[1]
    lines = feats * own // 128
    space = pl.BlockSpec(memory_space=pltpu.VMEM)
    return pl.pallas_call(
        functools.partial(scoped, PIECES),
        out_shape=(
            jax.ShapeDtypeStruct((rows, feats), F32),
            jax.ShapeDtypeStruct((lines, 128), F32),
            jax.ShapeDtypeStruct((lines, 128), F32),
        ),
        in_specs=[pl.BlockSpec(memory_space=pltpu.SMEM)] + [space] * 12,
        out_specs=(space,) * 3,
        scratch_shapes=[
            pltpu.VMEM((own, 2 * feats), BF16),
            pltpu.VMEM((own, 2 * feats), BF16),
            pltpu.VMEM((feats, own), BF16),
            pltpu.VMEM((feats, own), BF16),
            pltpu.VMEM((2, 6, 2 * own, rows), F32),
            pltpu.VMEM((2, 6, own, rows), BF16),
            pltpu.VMEM((own, rows), BF16),
            pltpu.VMEM((2, 6, feats, rows), BF16),
            pltpu.VMEM((feats, rows), F32),
            pltpu.VMEM((6, feats, rows), F32),
            pltpu.VMEM((own // 64, feats, 128), F32),
        ],
        compiler_params=pltpu.CompilerParams(vmem_limit_bytes=38 << 20),
        cost_estimate=pl.CostEstimate(
            flops=12 * 12 * rows * feats * own * 2, bytes_accessed=4 << 20, transcendentals=0
        ),
        name="sweep",
    )(core, *prepared, in_own, out_own, *pieces)


def per_device(states, cotangent, obs_count, step_index, step_table, w_in, b_hid, w_out, b_out):
    core = lax.axis_index("core")
    feats, own = w_in.shape
    part = own // 2
    bias = jnp.broadcast_to(b_hid[None, :], (8, own))
    odd = lax.axis_index("x") % 2
    layer = jnp.concatenate([jnp.where(core == 0, w_in, w_out), bias], axis=0)
    piece = jnp.where(odd == 0, layer[:, :part], layer[:, part:])
    arrived = swapped(piece, "par")
    prepared = prepare(
        obs_count, step_table, states, cotangent, step_index, w_in, w_out, bias, b_out[None, :]
    )
    near, prepared = lax.optimization_barrier((arrived, prepared))
    far = swapped(near, "x")
    pieces = (near, swapped(near, "core"), far, swapped(far, "core"))
    back, keep, send = run_sweep(core.reshape(1), prepared, w_in, w_out, pieces)
    keep, send = (v.reshape(feats // 2, 2 * own // 128, 128) for v in (keep, send))
    pair = (keep + swapped(send, "core")).astype(BF16)
    arrived = lax.all_to_all(pair, ("y", "z", "x"), split_axis=0, concat_axis=0, tiled=True)
    total = arrived.astype(F32).sum(axis=0).reshape(2, 1, own)
    return (back, total[0], total[1])


def solution(mesh):
    fine = Mesh(mesh.devices.reshape(SIZES), PLACE)
    return jax.shard_map(
        per_device,
        mesh=fine,
        in_specs=(
            P(SEQ, None),
            P(SEQ, None),
            P(SEQ),
            P(None, SEQ),
            P(),
            P(None, "par"),
            P("par"),
            P(None, "par"),
            P(),
        ),
        out_specs=(P(SEQ, None), P(SEQ, "par"), P(SEQ, "par")),
        check_vma=False,
    )
```

time: 70.3 us -> 64.5 us (0.917)
  blocking collectives: 29.8 us -> 23 us
  starting transfers between devices: 9.78 us -> 14.2 us
  Pallas kernels: 23 us -> 19.1 us
  waiting for transfers between devices: 2.43 us -> 5.34 us
  local copies, waits for them, and re-layouts: 2.82 us -> 0.66 us
    all_gather x2 -> x0, blocking collectives: 6.81 us -> none  [per_device(): near, far = (lax.all_gather(near, 'core'), lax.all_gather(far, 'core'))]
    pallas_call x1, Pallas kernels: 22.6 us -> 18.2 us  [run_sweep(): pl.pallas_call(functools.partial(scoped, PIECES), out_shape=(jax.ShapeDty...]
    ppermute x3 -> x5, starting transfers between devices: 9.78 us -> 14.2 us  [swapped(): return lax.ppermute(value, PLACE, pairs)]
    ppermute x3 -> x5, waiting for transfers between devices: 2.43 us -> 5.34 us  [swapped(): return lax.ppermute(value, PLACE, pairs)]
    unnamed x18, local copies, waits for them, and re-layouts: 2.14 us -> 0.05 us
  transfers between devices with their start and end apart: 3 -> 5, of which waited for: 2 -> 4; matrix products, arithmetic and copies ran while one was open for 0% -> 0% of each run, Pallas kernels for 1% -> 1%
where the time goes in v4:
time: 64.5 us; the launch traced here: 64.3 us
  blocking collectives  23 us (36%)
  Pallas kernels  19.1 us (30%)
  starting transfers between devices  14.2 us (22%)
  waiting for transfers between devices  5.34 us (8%)
  other arithmetic  1.21 us (2%)
  between operations  0.8 us (1%)
  local copies, waits for them, and re-layouts  0.66 us (1%)
    all_to_all x1, blocking collectives, per_device(): lax.all_to_all(pair, ('y', 'z', 'x'), split_axis=0, concat_axis=0, tiled=...  23 us
    pallas_call x1, Pallas kernels, run_sweep(): pl.pallas_call(functools.partial(scoped, PIECES), out_shape=(jax.ShapeDty...  18.2 us
    ppermute x5, starting transfers between devices, swapped(): return lax.ppermute(value, PLACE, pairs)  14.2 us
    ppermute x5, waiting for transfers between devices, swapped(): return lax.ppermute(value, PLACE, pairs)  5.34 us
  transfers between devices with their start and end apart: 5, of which 4 were waited for; matrix products, arithmetic and copies ran while one was open for 0% of the time, Pallas kernels for 1%

profile of v4, /device:TPU:1, one launch (start us, length us, event | category | flops | bytes accessed | tf_op | source)
XLA Modules:
  0.0 64.3 jit_solution(16652969153371846010)
XLA Ops:
  0.7 1.0 %broadcast_select_fusion = bf16[128,1024]{1,0:T(8,128)(2,1)S(1)} fusion(bf16[128,1024]{1,0:T(8,128)(2,1)} %refs_7_.1, bf16[128,1024]{1,0:T(8,128)(2,1)} %refs_8_.1, pred[]{:T(512)S(6)} %eq.9), kind=kLoop, calls=%fused_computation.4 | loop fusion | flops 131072 | bytes 786433 | tf_op jit(solution)/shard_map/jit(_where)/select_n | solution.py:348
  1.7 0.0 copy-done.8
  1.7 0.0 copy-start
  1.8 0.0 copy-start.2
  1.8 0.0 copy-start.4
  1.8 0.0 copy-start.5
  1.8 0.0 copy-start.6
  1.8 0.0 copy-start.7
  1.9 7.8 %collective-permute-start = (bf16[136,512]{1,0:T(8,128)(2,1)S(1)}, bf16[136,512]{1,0:T(8,128)(2,1)S(1)}, u32[]{:S(2)}, u32[]{:S(2)}) collective-permute-start(bf16[136,512]{1,0:T(8,128)(2,1)S(1)} %fusion.1), channel_id=1, source_target_pairs={{0,1},{1,0},{2,3},{3,2},{4,5},{5,4},{6,7},{7,6},{8,9},{9,8},{10,11... | collective-permute-start | bytes 417800 | tf_op jit(solution)/shard_map/ppermute | solution.py:24
  9.7 0.9 %prepare.1 = (f32[128,256]{1,0:T(8,128)S(1)}, f32[128,256]{1,0:T(8,128)S(1)}, f32[2,256]{1,0:T(2,128)S(1)}, bf16[1024,256]{1,0:T(8,128)(2,1)S(1)}, bf16[1024,256...) custom-call(s32[2]{0:T(128)S(1)} %copy-done.5, f32[16]{0:T(128)S(1)} %copy-done.6, f32[256,128]{1,0:T(8,128)S(1)} %copy-done.2, ...), custom_call_target="tpu_custom_call" | custom-call | flops 200000000 | bytes 2097152 | tf_op jit(solution)/shard_map/prepare/pallas_call | solution.py:91
  10.7 1.9 %collective-permute-done.refs_9_ = bf16[136,512]{1,0:T(8,128)(2,1)S(1)} collective-permute-done((bf16[136,512]{1,0:T(8,128)(2,1)S(1)}, bf16[136,512]{1,0:T(8,128)(2,1)S(1)}, u32[]{:S(2)}, u32[]{:S(2)}) %collective-permute-start) | collective-permute-done | bytes 139296 | tf_op jit(solution)/shard_map/ppermute | solution.py:24
  12.6 1.7 %collective-permute-start.2 = (bf16[136,512]{1,0:T(8,128)(2,1)S(1)}, bf16[136,512]{1,0:T(8,128)(2,1)S(1)}, u32[]{:S(2)}, u32[]{:S(2)}) collective-permute-start(bf16[136,512]{1,0:T(8,128)(2,1)S(1)} %collective-permute-done.refs_9_), channel_id=1, source_target_pairs={{0,4},{1,5},{2,6},{3,7},{4,0},{5,1},{6,2},{7,3},{8,12},{9,13},{10,... | collective-permute-start | bytes 417800 | tf_op jit(solution)/shard_map/ppermute | solution.py:24
  14.3 1.6 %collective-permute-start.1 = (bf16[136,512]{1,0:T(8,128)(2,1)S(1)}, bf16[136,512]{1,0:T(8,128)(2,1)S(1)}, u32[]{:S(2)}, u32[]{:S(2)}) collective-permute-start(bf16[136,512]{1,0:T(8,128)(2,1)S(1)} %collective-permute-done.refs_9_), channel_id=1, source_target_pairs={{0,2},{1,3},{2,0},{3,1},{4,6},{5,7},{6,4},{7,5},{8,10},{9,11},{10,... | collective-permute-start | bytes 417800 | tf_op jit(solution)/shard_map/ppermute | solution.py:24
  15.9 0.8 %collective-permute-done.2.refs_11_ = bf16[136,512]{1,0:T(8,128)(2,1)S(1)} collective-permute-done((bf16[136,512]{1,0:T(8,128)(2,1)S(1)}, bf16[136,512]{1,0:T(8,128)(2,1)S(1)}, u32[]{:S(2)}, u32[]{:S(2)}) %collective-permute-start.2) | collective-permute-done | bytes 139296 | tf_op jit(solution)/shard_map/ppermute | solution.py:24
  16.7 2.8 %collective-permute-start.3 = (bf16[136,512]{1,0:T(8,128)(2,1)S(1)}, bf16[136,512]{1,0:T(8,128)(2,1)S(1)}, u32[]{:S(2)}, u32[]{:S(2)}) collective-permute-start(bf16[136,512]{1,0:T(8,128)(2,1)S(1)} %collective-permute-done.2.refs_11_), channel_id=1, source_target_pairs={{0,2},{1,3},{2,0},{3,1},{4,6},{5,7},{6,4},{7,5},{8,10},{9,11},{10,... | collective-permute-start | bytes 417800 | tf_op jit(solution)/shard_map/ppermute | solution.py:24
  19.5 0.0 collective-permute-done.1.refs_10_
  19.5 1.0 %collective-permute-done.3.refs_12_ = bf16[136,512]{1,0:T(8,128)(2,1)S(1)} collective-permute-done((bf16[136,512]{1,0:T(8,128)(2,1)S(1)}, bf16[136,512]{1,0:T(8,128)(2,1)S(1)}, u32[]{:S(2)}, u32[]{:S(2)}) %collective-permute-start.3) | collective-permute-done | bytes 139296 | tf_op jit(solution)/shard_map/ppermute | solution.py:24
  20.5 18.2 %sweep.1 = (f32[256,128]{1,0:T(8,128)}, f32[1024,128]{1,0:T(8,128)S(1)}, f32[1024,128]{1,0:T(8,128)S(1)}) custom-call(s32[1]{0:T(128)} %bitcast.refs_0_, f32[128,256]{1,0:T(8,128)S(1)} %get-tuple-element.25.refs_1_, f32[128,256]{1,0:T(8,128)S(1)} %get-tuple-element.26.refs_2_, f32[2,256]{1,0:T(2,128)S(1)} %get-tuple-element.27.refs_3_, ...), custom_call_target="tpu_custom_call" | custom-call | flops 9663676416 | bytes 4194304 | tf_op jit(solution)/shard_map/sweep/pallas_call | solution.py:312
  38.6 0.3 collective-permute-start.4
  38.9 1.6 %collective-permute-done.4 = f32[64,16,128]{2,1,0:T(8,128)S(1)} collective-permute-done((f32[64,16,128]{2,1,0:T(8,128)S(1)}, f32[64,16,128]{2,1,0:T(8,128)S(1)}, u32[]{:S(2)}, u32[]{:S(2)}) %collective-permute-start.4) | collective-permute-done | bytes 524320 | tf_op jit(solution)/shard_map/ppermute | solution.py:24
  40.6 0.1 add_convert_fusion
  40.6 23.0 %all_to_all.5 = bf16[64,16,128]{2,1,0:T(8,128)(2,1)S(1)} all-to-all(bf16[64,16,128]{2,1,0:T(8,128)(2,1)S(1)} %add_convert_fusion), channel_id=1, replica_groups=mesh['y'=4,'z'=4,'x'=4,'core'=2,'par'=2] {'y','z','x'}, dimensions={0} | all-to-all | bytes 524288 | tf_op jit(solution)/shard_map/all_to_all | solution.py:360
  63.7 0.1 convert_reduce_fusion
  63.7 0.6 fusion.2
  (13 shorter events, 0.1 us)
Async XLA Ops:
  0.6 1.1 %copy-start.8 = (bf16[1024]{0:T(1024)(128)(2,1)S(1)}, bf16[1024]{0:T(1024)(128)(2,1)}, u32[]{:S(2)}) copy-start(bf16[1024]{0:T(1024)(128)(2,1)} %param.15) | copy-start | bytes 6148
  0.7 9.0 %copy-start.1 = (bf16[128,1024]{1,0:T(8,128)(2,1)S(1)}, bf16[128,1024]{1,0:T(8,128)(2,1)}, u32[]{:S(2)}) copy-start(bf16[128,1024]{1,0:T(8,128)(2,1)} %refs_8_.1) | copy-start | bytes 786436
  0.7 9.0 %copy-start.3 = (f32[256,128]{1,0:T(8,128)S(1)}, f32[256,128]{1,0:T(8,128)}, u32[]{:S(2)}) copy-start(f32[256,128]{1,0:T(8,128)} %cotangent.1) | copy-start | bytes 393220
  1.7 8.0 %copy-start = (bf16[128,1024]{1,0:T(8,128)(2,1)S(1)}, bf16[128,1024]{1,0:T(8,128)(2,1)}, u32[]{:S(2)}) copy-start(bf16[128,1024]{1,0:T(8,128)(2,1)} %refs_7_.1) | copy-start | bytes 786436
  1.8 7.9 %copy-start.2 = (f32[256,128]{1,0:T(8,128)S(1)}, f32[256,128]{1,0:T(8,128)}, u32[]{:S(2)}) copy-start(f32[256,128]{1,0:T(8,128)} %states.1) | copy-start | bytes 393220
  1.8 7.9 %copy-start.4 = (s32[2,256]{1,0:T(2,128)S(1)}, s32[2,256]{1,0:T(2,128)}, u32[]{:S(2)}) copy-start(s32[2,256]{1,0:T(2,128)} %index.1) | copy-start | bytes 6148
  1.8 7.9 %copy-start.5 = (s32[2]{0:T(128)S(1)}, s32[2]{0:T(128)}, u32[]{:S(2)}) copy-start(s32[2]{0:T(128)} %counts.1) | copy-start | bytes 28
  1.8 7.9 %copy-start.6 = (f32[16]{0:T(128)S(1)}, f32[16]{0:T(128)}, u32[]{:S(2)}) copy-start(f32[16]{0:T(128)} %table.1) | copy-start | bytes 196
  1.8 7.9 %copy-start.7 = (f32[128]{0:T(128)S(1)}, f32[128]{0:T(128)}, u32[]{:S(2)}) copy-start(f32[128]{0:T(128)} %param.17) | copy-start | bytes 1540
  1.9 10.7 %collective-permute-start = (bf16[136,512]{1,0:T(8,128)(2,1)S(1)}, bf16[136,512]{1,0:T(8,128)(2,1)S(1)}, u32[]{:S(2)}, u32[]{:S(2)}) collective-permute-start(bf16[136,512]{1,0:T(8,128)(2,1)S(1)} %fusion.1), channel_id=1, source_target_pairs={{0,1},{1,0},{2,3},{3,2},{4,5},{5,4},{6,7},{7,6},{8,9},{9,8},{10,11... | collective-permute-start | bytes 417800 | tf_op jit(solution)/shard_map/ppermute | solution.py:24
  12.6 4.1 %collective-permute-start.2 = (bf16[136,512]{1,0:T(8,128)(2,1)S(1)}, bf16[136,512]{1,0:T(8,128)(2,1)S(1)}, u32[]{:S(2)}, u32[]{:S(2)}) collective-permute-start(bf16[136,512]{1,0:T(8,128)(2,1)S(1)} %collective-permute-done.refs_9_), channel_id=1, source_target_pairs={{0,4},{1,5},{2,6},{3,7},{4,0},{5,1},{6,2},{7,3},{8,12},{9,13},{10,... | collective-permute-start | bytes 417800 | tf_op jit(solution)/shard_map/ppermute | solution.py:24
  14.3 5.2 %collective-permute-start.1 = (bf16[136,512]{1,0:T(8,128)(2,1)S(1)}, bf16[136,512]{1,0:T(8,128)(2,1)S(1)}, u32[]{:S(2)}, u32[]{:S(2)}) collective-permute-start(bf16[136,512]{1,0:T(8,128)(2,1)S(1)} %collective-permute-done.refs_9_), channel_id=1, source_target_pairs={{0,2},{1,3},{2,0},{3,1},{4,6},{5,7},{6,4},{7,5},{8,10},{9,11},{10,... | collective-permute-start | bytes 417800 | tf_op jit(solution)/shard_map/ppermute | solution.py:24
  16.7 3.8 %collective-permute-start.3 = (bf16[136,512]{1,0:T(8,128)(2,1)S(1)}, bf16[136,512]{1,0:T(8,128)(2,1)S(1)}, u32[]{:S(2)}, u32[]{:S(2)}) collective-permute-start(bf16[136,512]{1,0:T(8,128)(2,1)S(1)} %collective-permute-done.2.refs_11_), channel_id=1, source_target_pairs={{0,2},{1,3},{2,0},{3,1},{4,6},{5,7},{6,4},{7,5},{8,10},{9,11},{10,... | collective-permute-start | bytes 417800 | tf_op jit(solution)/shard_map/ppermute | solution.py:24
  38.6 1.9 %collective-permute-start.4 = (f32[64,16,128]{2,1,0:T(8,128)S(1)}, f32[64,16,128]{2,1,0:T(8,128)S(1)}, u32[]{:S(2)}, u32[]{:S(2)}) collective-permute-start(f32[64,16,128]{2,1,0:T(8,128)S(1)} %bitcast.8), channel_id=1, source_target_pairs={{0,2},{1,3},{2,0},{3,1},{4,6},{5,7},{6,4},{7,5},{8,10},{9,11},{10,... | collective-permute-start | bytes 1572872 | tf_op jit(solution)/shard_map/ppermute | solution.py:24

commit v5 on v4

--- a/solution.py
+++ b/solution.py
@@ -14,14 +14,20 @@
 SIZES = (4, 4, 4, 2, 2)
 
 
-def swapped(value, axis):
-    at = PLACE.index(axis)
+def sent(value, other_place):
     pairs = []
     for source in range(int(np.prod(SIZES))):
-        place = list(np.unravel_index(source, SIZES))
-        place[at] ^= 1
-        pairs.append((source, int(np.ravel_multi_index(place, SIZES))))
+        place = [int(v) for v in np.unravel_index(source, SIZES)]
+        pairs.append((source, int(np.ravel_multi_index(other_place(*place), SIZES))))
     return lax.ppermute(value, PLACE, pairs)
+
+
+def other_core(y, z, x, core, par):
+    return y, z, x, 1 - core, par
+
+
+def other_half(y, z, x, core, par):
+    return y, SIZES[1] - 1 - z, x, core, 1 - par
 
 
 COEF_A = [
@@ -54,15 +60,11 @@
     return jnp.concatenate([square.T, low.T.astype(BF16)], axis=1)
 
 
-def turned_out(square):
-    return jnp.concatenate([square.T, jnp.zeros((128, 128), BF16)], axis=1)
-
-
 def prepare_kernel(
-    counts, table, states, cotangent, index, w_in, w_out, bias, b_out,
+    counts, table, states, cotangent, index, w_in, w_out, layer, b_out,
     states_t, initial_t, sizes, in_t, out_t, bias_t,
 ):
-    rows = states.shape[0]
+    rows, feats = states.shape
     states_t[...] = transposed(states[...])
     slot = lax.broadcasted_iota(jnp.int32, (1, rows), 1)
     slots = rows // counts.shape[0]
@@ -80,11 +82,11 @@
     bias_t[...] = jnp.concatenate([column, column], axis=1)
     for at in range(0, w_in.shape[1], 128):
         here = slice(at, at + 128)
-        in_t[here] = turned_in(w_in[:, here], bias[:, here])
-        out_t[here] = turned_out(w_out[:, here])
-
-
-def prepare(counts, table, states, cotangent, index, w_in, w_out, bias, b_out):
+        in_t[here] = turned_in(w_in[:, here], layer[feats:, here])
+        out_t[here] = w_out[:, here].T
+
+
+def prepare(counts, table, states, cotangent, index, w_in, w_out, layer, b_out):
     rows, feats = states.shape
     own = w_in.shape[1]
     space = pl.BlockSpec(memory_space=pltpu.VMEM)
@@ -95,7 +97,7 @@
             jax.ShapeDtypeStruct((feats, rows), F32),
             jax.ShapeDtypeStruct(index.shape, F32),
             jax.ShapeDtypeStruct((own, 2 * feats), BF16),
-            jax.ShapeDtypeStruct((own, 2 * feats), BF16),
+            jax.ShapeDtypeStruct((own, feats), BF16),
             jax.ShapeDtypeStruct((feats, rows), F32),
         ),
         in_specs=[pl.BlockSpec(memory_space=pltpu.SMEM)] * 2 + [space] * 7,
@@ -103,30 +105,27 @@
         compiler_params=pltpu.CompilerParams(vmem_limit_bytes=8 << 20),
         cost_estimate=pl.CostEstimate(flops=200_000_000, bytes_accessed=2 << 20, transcendentals=0),
         name="prepare",
-    )(counts, table, states, cotangent, index, w_in, w_out, bias, b_out)
+    )(counts, table, states, cotangent, index, w_in, w_out, layer, b_out)
 
 
 def sweep_kernel(
     core, states_t, initial_t, sizes, in_t_own, out_t_own, bias_t, in_own, out_own,
-    near, near_peer, far, far_peer,
+    near, near_peer,
     back, keep, send,
     in_t_other, out_t_other, in_other, out_other, hid, hid_own, inner_own, probe, value, terms, grads,
     *accumulators,
 ):
     feats, own = in_own.shape
     rows = states_t.shape[1]
-    part = near.shape[1]
-    tiles = 2 * own // TILE
     first_core = core[0] == 0
-    for start, mine, peer in ((0, near, near_peer), (part, far, far_peer)):
-        for at in range(0, part, 128):
-            here, to = slice(at, at + 128), slice(start + at, start + at + 128)
-            a, b = mine[:feats, here], peer[:feats, here]
-            square_in, square_out = jnp.where(first_core, a, b), jnp.where(first_core, b, a)
-            in_other[:, to] = square_in
-            out_other[:, to] = square_out
-            in_t_other[to] = turned_in(square_in, mine[feats:, here])
-            out_t_other[to] = turned_out(square_out)
+    for at in range(0, own, 128):
+        here = slice(at, at + 128)
+        a, b = near[:feats, here], near_peer[:feats, here]
+        square_in, square_out = jnp.where(first_core, a, b), jnp.where(first_core, b, a)
+        in_other[:, here] = square_in
+        out_other[:, here] = square_out
+        in_t_other[here] = turned_in(square_in, near[feats:, here])
+        out_t_other[here] = square_out.T
     grads[...] = jnp.zeros_like(grads)
     unit = jnp.where(lax.broadcasted_iota(jnp.int32, (feats, rows), 0) == 0, 1.0, 0.0).astype(BF16)
     nothing = jnp.zeros((feats, rows), BF16)
@@ -153,9 +152,10 @@
 
     def stream(weights, q, piece, register):
         at = place(q, piece // 2) + piece % 2 * PIECE
-        pltpu.matmul_acc_lhs(
-            slot(q, piece), lines(*weights, at, PIECE), load_staged_rhs=register
-        )
+        taken = lines(*weights, at, PIECE)
+        if taken.shape[1] < TILE:
+            taken = jnp.concatenate([taken, nothing[:, : TILE - taken.shape[1]]], axis=1)
+        pltpu.matmul_acc_lhs(slot(q, piece), taken, load_staged_rhs=register)
 
     def forward(step, _):
         size = sizes[pl.ds(step, 1), :]
@@ -316,11 +316,11 @@
             jax.ShapeDtypeStruct((lines, 128), F32),
             jax.ShapeDtypeStruct((lines, 128), F32),
         ),
-        in_specs=[pl.BlockSpec(memory_space=pltpu.SMEM)] + [space] * 12,
+        in_specs=[pl.BlockSpec(memory_space=pltpu.SMEM)] + [space] * 10,
         out_specs=(space,) * 3,
         scratch_shapes=[
             pltpu.VMEM((own, 2 * feats), BF16),
-            pltpu.VMEM((own, 2 * feats), BF16),
+            pltpu.VMEM((own, feats), BF16),
             pltpu.VMEM((feats, own), BF16),
             pltpu.VMEM((feats, own), BF16),
             pltpu.VMEM((2, 6, 2 * own, rows), F32),
@@ -343,20 +343,18 @@
     core = lax.axis_index("core")
     feats, own = w_in.shape
     part = own // 2
-    bias = jnp.broadcast_to(b_hid[None, :], (8, own))
-    odd = lax.axis_index("x") % 2
-    layer = jnp.concatenate([jnp.where(core == 0, w_in, w_out), bias], axis=0)
-    piece = jnp.where(odd == 0, layer[:, :part], layer[:, part:])
-    arrived = swapped(piece, "par")
+    layer = jnp.concatenate(
+        [jnp.where(core == 0, w_in, w_out), jnp.broadcast_to(b_hid[None, :], (8, own))], axis=0
+    )
+    arrived = sent(layer, other_half)
     prepared = prepare(
-        obs_count, step_table, states, cotangent, step_index, w_in, w_out, bias, b_out[None, :]
+        obs_count, step_table, states, cotangent, step_index, w_in, w_out, layer, b_out[None, :]
     )
     near, prepared = lax.optimization_barrier((arrived, prepared))
-    far = swapped(near, "x")
-    pieces = (near, swapped(near, "core"), far, swapped(far, "core"))
+    pieces = (near, sent(near, other_core))
     back, keep, send = run_sweep(core.reshape(1), prepared, w_in, w_out, pieces)
     keep, send = (v.reshape(feats // 2, 2 * own // 128, 128) for v in (keep, send))
-    pair = (keep + swapped(send, "core")).astype(BF16)
+    pair = (keep + sent(send, other_core)).astype(BF16)
     arrived = lax.all_to_all(pair, ("y", "z", "x"), split_axis=0, concat_axis=0, tiled=True)
     total = arrived.astype(F32).sum(axis=0).reshape(2, 1, own)
     return (back, total[0], total[1])

time: 64.5 us -> 64.1 us (level)
  waiting for transfers between devices: 5.34 us -> 14.4 us
  starting transfers between devices: 14.2 us -> 7.74 us
  blocking collectives: 23 us -> 20.2 us
    ppermute x5 -> x3, waiting for transfers between devices: 5.34 us -> 14.4 us  [sent(): return lax.ppermute(value, PLACE, pairs)]
    ppermute x5 -> x3, starting transfers between devices: 14.2 us -> 7.74 us  [sent(): return lax.ppermute(value, PLACE, pairs)]
    all_to_all x1, blocking collectives: 23 us -> 20.2 us  [per_device(): lax.all_to_all(pair, ('y', 'z', 'x'), split_axis=0, concat_axis=0, tiled=...]
  transfers between devices with their start and end apart: 5 -> 3, of which waited for: 4 -> 3; matrix products, arithmetic and copies ran while one was open for 0% -> 0% of each run, Pallas kernels for 1% -> 1%
where the time goes in v5:
time: 64.1 us; the launch traced here: 63.9 us
  blocking collectives  20.2 us (32%)
  Pallas kernels  19 us (30%)
  waiting for transfers between devices  14.4 us (22%)
  starting transfers between devices  7.74 us (12%)
  other arithmetic  1.2 us (2%)
  between operations  0.79 us (1%)
  local copies, waits for them, and re-layouts  0.66 us (1%)
    all_to_all x1, blocking collectives, per_device(): lax.all_to_all(pair, ('y', 'z', 'x'), split_axis=0, concat_axis=0, tiled=...  20.2 us
    pallas_call x1, Pallas kernels, run_sweep(): pl.pallas_call(functools.partial(scoped, PIECES), out_shape=(jax.ShapeDty...  18 us
    ppermute x3, waiting for transfers between devices, sent(): return lax.ppermute(value, PLACE, pairs)  14.4 us
    ppermute x3, starting transfers between devices, sent(): return lax.ppermute(value, PLACE, pairs)  7.74 us
  transfers between devices with their start and end apart: 3, of which 3 were waited for; matrix products, arithmetic and copies ran while one was open for 0% of the time, Pallas kernels for 1%

profile of v5, /device:TPU:1, one launch (start us, length us, event | category | flops | bytes accessed | tf_op | source)
XLA Modules:
  0.0 63.9 jit_solution(4044508387283471678)
XLA Ops:
  0.6 0.0 copy-start.8
  0.6 0.0 copy-start.2
  0.7 0.0 copy-start.3
  0.7 1.0 %broadcast_select_fusion = bf16[128,1024]{1,0:T(8,128)(2,1)S(1)} fusion(bf16[128,1024]{1,0:T(8,128)(2,1)} %refs_7_.1, bf16[128,1024]{1,0:T(8,128)(2,1)} %refs_8_.1, pred[]{:T(512)S(6)} %eq.3), kind=kLoop, calls=%fused_computation.3 | loop fusion | flops 131072 | bytes 786433 | tf_op jit(solution)/shard_map/jit(_where)/select_n | solution.py:347
  1.7 0.0 copy-done.8
  1.7 0.0 copy-start
  1.7 0.0 copy-start.1
  1.8 0.0 copy-start.4
  1.8 0.0 copy-start.5
  1.8 0.0 copy-start.6
  1.8 0.0 copy-start.7
  1.8 6.5 %collective-permute-start = (bf16[136,1024]{1,0:T(8,128)(2,1)S(1)}, bf16[136,1024]{1,0:T(8,128)(2,1)S(1)}, u32[]{:S(2)}, u32[]{:S(2)}) collective-permute-start(bf16[136,1024]{1,0:T(8,128)(2,1)S(1)} %pad_maximum_fusion.layer), channel_id=1, source_target_pairs={{0,49},{1,48},{2,51},{3,50},{4,53},{5,52},{6,55},{7,54},{8,57},{9,... | collective-permute-start | bytes 835592 | tf_op jit(solution)/shard_map/ppermute | solution.py:22
  8.3 0.0 copy-done.2
  8.4 0.9 %prepare.1 = (f32[128,256]{1,0:T(8,128)S(1)}, f32[128,256]{1,0:T(8,128)S(1)}, f32[2,256]{1,0:T(2,128)S(1)}, bf16[1024,256]{1,0:T(8,128)(2,1)S(1)}, bf16[1024,128...) custom-call(s32[2]{0:T(128)S(1)} %copy-done.5, f32[16]{0:T(128)S(1)} %copy-done.6, f32[256,128]{1,0:T(8,128)S(1)} %copy-done.2, ...), custom_call_target="tpu_custom_call" | custom-call | flops 200000000 | bytes 2097152 | tf_op jit(solution)/shard_map/prepare/pallas_call | solution.py:93
  9.3 11.6 %collective-permute-done.refs_9_ = bf16[136,1024]{1,0:T(8,128)(2,1)S(1)} collective-permute-done((bf16[136,1024]{1,0:T(8,128)(2,1)S(1)}, bf16[136,1024]{1,0:T(8,128)(2,1)S(1)}, u32[]{:S(2)}, u32[]{:S(2)}) %collective-permute-start) | collective-permute-done | bytes 278560 | tf_op jit(solution)/shard_map/ppermute | solution.py:22
  21.0 0.9 %collective-permute-start.1 = (bf16[136,1024]{1,0:T(8,128)(2,1)S(1)}, bf16[136,1024]{1,0:T(8,128)(2,1)S(1)}, u32[]{:S(2)}, u32[]{:S(2)}) collective-permute-start(bf16[136,1024]{1,0:T(8,128)(2,1)S(1)} %collective-permute-done.refs_9_), channel_id=1, source_target_pairs={{0,2},{1,3},{2,0},{3,1},{4,6},{5,7},{6,4},{7,5},{8,10},{9,11},{10,... | collective-permute-start | bytes 835592 | tf_op jit(solution)/shard_map/ppermute | solution.py:22
  21.9 1.2 %collective-permute-done.1.refs_10_ = bf16[136,1024]{1,0:T(8,128)(2,1)S(1)} collective-permute-done((bf16[136,1024]{1,0:T(8,128)(2,1)S(1)}, bf16[136,1024]{1,0:T(8,128)(2,1)S(1)}, u32[]{:S(2)}, u32[]{:S(2)}) %collective-permute-start.1) | collective-permute-done | bytes 278560 | tf_op jit(solution)/shard_map/ppermute | solution.py:22
  23.1 18.0 %sweep.1 = (f32[256,128]{1,0:T(8,128)}, f32[1024,128]{1,0:T(8,128)S(1)}, f32[1024,128]{1,0:T(8,128)S(1)}) custom-call(s32[1]{0:T(128)} %bitcast.refs_0_, f32[128,256]{1,0:T(8,128)S(1)} %get-tuple-element.25.refs_1_, f32[128,256]{1,0:T(8,128)S(1)} %get-tuple-element.26.refs_2_, f32[2,256]{1,0:T(2,128)S(1)} %get-tuple-element.27.refs_3_, ...), custom_call_target="tpu_custom_call" | custom-call | flops 9663676416 | bytes 4194304 | tf_op jit(solution)/shard_map/sweep/pallas_call | solution.py:312
  41.1 0.3 collective-permute-start.2
  41.4 1.6 %collective-permute-done.2 = f32[64,16,128]{2,1,0:T(8,128)S(1)} collective-permute-done((f32[64,16,128]{2,1,0:T(8,128)S(1)}, f32[64,16,128]{2,1,0:T(8,128)S(1)}, u32[]{:S(2)}, u32[]{:S(2)}) %collective-permute-start.2) | collective-permute-done | bytes 524320 | tf_op jit(solution)/shard_map/ppermute | solution.py:22
  43.0 0.1 add_convert_fusion
  43.1 20.2 %all_to_all.5 = bf16[64,16,128]{2,1,0:T(8,128)(2,1)S(1)} all-to-all(bf16[64,16,128]{2,1,0:T(8,128)(2,1)S(1)} %add_convert_fusion), channel_id=1, replica_groups=mesh['y'=4,'z'=4,'x'=4,'core'=2,'par'=2] {'y','z','x'}, dimensions={0} | all-to-all | bytes 524288 | tf_op jit(solution)/shard_map/all_to_all | solution.py:358
  63.2 0.1 convert_reduce_fusion
  63.3 0.6 fusion
  (9 shorter events, 0.0 us)
Async XLA Ops:
  0.6 1.1 %copy-start.8 = (bf16[1024]{0:T(1024)(128)(2,1)S(1)}, bf16[1024]{0:T(1024)(128)(2,1)}, u32[]{:S(2)}) copy-start(bf16[1024]{0:T(1024)(128)(2,1)} %param.15) | copy-start | bytes 6148
  0.6 7.7 %copy-start.2 = (f32[256,128]{1,0:T(8,128)S(1)}, f32[256,128]{1,0:T(8,128)}, u32[]{:S(2)}) copy-start(f32[256,128]{1,0:T(8,128)} %states.1) | copy-start | bytes 393220
  0.7 7.7 %copy-start.3 = (f32[256,128]{1,0:T(8,128)S(1)}, f32[256,128]{1,0:T(8,128)}, u32[]{:S(2)}) copy-start(f32[256,128]{1,0:T(8,128)} %cotangent.1) | copy-start | bytes 393220
  1.7 6.6 %copy-start = (bf16[128,1024]{1,0:T(8,128)(2,1)S(1)}, bf16[128,1024]{1,0:T(8,128)(2,1)}, u32[]{:S(2)}) copy-start(bf16[128,1024]{1,0:T(8,128)(2,1)} %refs_7_.1) | copy-start | bytes 786436
  1.7 6.6 %copy-start.1 = (bf16[128,1024]{1,0:T(8,128)(2,1)S(1)}, bf16[128,1024]{1,0:T(8,128)(2,1)}, u32[]{:S(2)}) copy-start(bf16[128,1024]{1,0:T(8,128)(2,1)} %refs_8_.1) | copy-start | bytes 786436
  1.8 6.6 %copy-start.4 = (s32[2,256]{1,0:T(2,128)S(1)}, s32[2,256]{1,0:T(2,128)}, u32[]{:S(2)}) copy-start(s32[2,256]{1,0:T(2,128)} %index.1) | copy-start | bytes 6148
  1.8 6.5 %copy-start.5 = (s32[2]{0:T(128)S(1)}, s32[2]{0:T(128)}, u32[]{:S(2)}) copy-start(s32[2]{0:T(128)} %counts.1) | copy-start | bytes 28
  1.8 6.5 %copy-start.6 = (f32[16]{0:T(128)S(1)}, f32[16]{0:T(128)}, u32[]{:S(2)}) copy-start(f32[16]{0:T(128)} %table.1) | copy-start | bytes 196
  1.8 6.5 %copy-start.7 = (f32[128]{0:T(128)S(1)}, f32[128]{0:T(128)}, u32[]{:S(2)}) copy-start(f32[128]{0:T(128)} %param.17) | copy-start | bytes 1540
  1.8 19.1 %collective-permute-start = (bf16[136,1024]{1,0:T(8,128)(2,1)S(1)}, bf16[136,1024]{1,0:T(8,128)(2,1)S(1)}, u32[]{:S(2)}, u32[]{:S(2)}) collective-permute-start(bf16[136,1024]{1,0:T(8,128)(2,1)S(1)} %pad_maximum_fusion.layer), channel_id=1, source_target_pairs={{0,49},{1,48},{2,51},{3,50},{4,53},{5,52},{6,55},{7,54},{8,57},{9,... | collective-permute-start | bytes 835592 | tf_op jit(solution)/shard_map/ppermute | solution.py:22
  21.0 2.1 %collective-permute-start.1 = (bf16[136,1024]{1,0:T(8,128)(2,1)S(1)}, bf16[136,1024]{1,0:T(8,128)(2,1)S(1)}, u32[]{:S(2)}, u32[]{:S(2)}) collective-permute-start(bf16[136,1024]{1,0:T(8,128)(2,1)S(1)} %collective-permute-done.refs_9_), channel_id=1, source_target_pairs={{0,2},{1,3},{2,0},{3,1},{4,6},{5,7},{6,4},{7,5},{8,10},{9,11},{10,... | collective-permute-start | bytes 835592 | tf_op jit(solution)/shard_map/ppermute | solution.py:22
  41.1 1.9 %collective-permute-start.2 = (f32[64,16,128]{2,1,0:T(8,128)S(1)}, f32[64,16,128]{2,1,0:T(8,128)S(1)}, u32[]{:S(2)}, u32[]{:S(2)}) collective-permute-start(f32[64,16,128]{2,1,0:T(8,128)S(1)} %bitcast.8), channel_id=1, source_target_pairs={{0,2},{1,3},{2,0},{3,1},{4,6},{5,7},{6,4},{7,5},{8,10},{9,11},{10,... | collective-permute-start | bytes 1572872 | tf_op jit(solution)/shard_map/ppermute | solution.py:22
